TPU v7x, 32 devices: a whole 2x2x4 slice. The times are simulated.
32 devices in a mesh: gx: 4 (over z), gy: 8 (over y, x, core).
Axes of the slice: x: 2, y: 2, z: 4, core: 2. Of those that a mesh axis runs over, the one named last changes fastest.
Arguments:
- rock_class: int32 [32, 128, 128], P('gx', 'gy'), may hold values from 0 to 15
- well_mask: int32 [32, 128, 128], P('gx', 'gy'), may hold values 0 or 1
- perm_table: float32 [16], replicated, may hold values from 0.01 to 1
- poro_table: float32 [16], replicated, may hold values from 0.05 to 0.35
- accum: float32 [3, 3, 32, 128, 128], P(None, None, 'gx', 'gy'), may hold values from -0.6 to 2, as said below
- mobility: float32 [3, 32, 128, 128], P(None, 'gx', 'gy'), may hold values from 0.2 to 2
- right_side: float32 [3, 32, 128, 128], P(None, 'gx', 'gy'), may hold values from -30 to 30
Outputs:
- pressure: float32 [32, 128, 128], P('gx', 'gy')
- correction: float32 [3, 32, 128, 128], P(None, 'gx', 'gy')
Inputs may be any that keep to these rules, and one draw needn't show every extreme that they name: `accum`: in each cell's 3 x 3 block the diagonal entries are positive and every off-diagonal entry is at most 0.3 times its row's diagonal entry in magnitude.
All inputs are finite; a program needn't handle non-finite values. No bound on the sum of `well_mask` on one device may be relied on, other than what follows from the above.
Results may differ from a plain program's by a relative error of at most 0.0001.
Values sent between devices are 32-bit elements; how exact they have to be, the bound alone decides.
No kernel may reach another device: no remote copies, remote signals or barrier semaphores. Data moves between devices by JAX's collectives and lax.ppermute only.
A program may use at most 64 MiB of HBM per device.

v0:
```python
import jax
import jax.numpy as jnp
from jax import lax
from jax.sharding import PartitionSpec as P

ITERS = 3


FACE_X = 1.0
FACE_Y = 1.0
FACE_Z = 2.0
WELL_FACTOR = 4.0


def padded_2(value, sides, width):
    for axis, dim in sides:
        devices, length = (lax.axis_size(axis), value.shape[dim])
        up = [(i, (i + 1) % devices) for i in range(devices - 1)]
        down = [(j, i) for i, j in up]
        last = lax.slice_in_dim(value, length - width, length, axis=dim)
        initial = lax.slice_in_dim(value, 0, width, axis=dim)
        before = lax.ppermute(last, axis, up)
        after = lax.ppermute(initial, axis, down)
        value = jnp.concatenate([before, value, after], axis=dim)
    return value


def harmonic(left_perm, right_perm, left_safe, right_safe):
    return 2.0 * left_perm * right_perm / (left_safe + right_safe)


def couplings(perm_ext, safe_ext, mobility_ext):
    row_perm = perm_ext[:, 1:-1]
    row_safe = safe_ext[:, 1:-1]
    row_mobility = mobility_ext[:, :, 1:-1]
    cross_x = (
        FACE_X
        * harmonic(row_perm[:-1], row_perm[1:], row_safe[:-1], row_safe[1:])
        * 0.5
        * (row_mobility[:, :-1] + row_mobility[:, 1:])
    )
    column_perm = perm_ext[1:-1]
    column_safe = safe_ext[1:-1]
    column_mobility = mobility_ext[:, 1:-1]
    cross_y = (
        FACE_Y
        * harmonic(column_perm[:, :-1], column_perm[:, 1:], column_safe[:, :-1], column_safe[:, 1:])
        * 0.5
        * (column_mobility[:, :, :-1] + column_mobility[:, :, 1:])
    )
    center_perm = perm_ext[1:-1, 1:-1]
    center_safe = safe_ext[1:-1, 1:-1]
    center_mobility = mobility_ext[:, 1:-1, 1:-1]
    vertical = (
        FACE_Z
        * harmonic(
            center_perm[:, :, :-1],
            center_perm[:, :, 1:],
            center_safe[:, :, :-1],
            center_safe[:, :, 1:],
        )
        * 0.5
        * (center_mobility[..., :-1] + center_mobility[..., 1:])
    )
    closed = jnp.zeros(vertical.shape[:-1] + (1,), jnp.float32)
    cross_z = jnp.concatenate([closed, vertical, closed], axis=-1)
    return (cross_x, cross_y, cross_z)


def face_flux(coupling, field_ext):
    cross_x, cross_y, cross_z = coupling
    center = field_ext[..., 1:-1, 1:-1, :]
    closed = jnp.zeros_like(center[..., :1])
    lifted = jnp.concatenate([closed, center, closed], axis=-1)
    totals = cross_x[..., 1:, :, :] * (center - field_ext[..., 2:, 1:-1, :])
    totals = totals + cross_x[..., :-1, :, :] * (center - field_ext[..., :-2, 1:-1, :])
    totals = totals + cross_y[..., :, 1:, :] * (center - field_ext[..., 1:-1, 2:, :])
    totals = totals + cross_y[..., :, :-1, :] * (center - field_ext[..., 1:-1, :-2, :])
    totals = totals + cross_z[..., 1:] * (center - lifted[..., 2:])
    totals = totals + cross_z[..., :-1] * (center - lifted[..., :-2])
    return totals


def phase_diagonal(coupling):
    cross_x, cross_y, cross_z = coupling
    totals = cross_x[..., 1:, :, :] + cross_x[..., :-1, :, :]
    totals = totals + cross_y[..., :, 1:, :] + cross_y[..., :, :-1, :]
    return totals + cross_z[..., 1:] + cross_z[..., :-1]


def identity_blocks():
    return jnp.eye(3, dtype=jnp.float32)[:, :, None, None, None]


def invert_blocks(blocks):

    def cofactor(row_index, column_index):
        next_row = (row_index + 1) % 3
        last_row = (row_index + 2) % 3
        next_col = (column_index + 1) % 3
        last_col = (column_index + 2) % 3
        return (
            blocks[next_row, next_col] * blocks[last_row, last_col]
            - blocks[next_row, last_col] * blocks[last_row, next_col]
        )

    adjugate = jnp.stack(
        [
            jnp.stack([cofactor(column_index, row_index) for column_index in range(3)])
            for row_index in range(3)
        ]
    )
    determinant = jnp.sum(blocks[0] * adjugate[:, 0], axis=0)
    return adjugate / determinant


def jacobian(storage_block, coupling, phase_well, center, field_ext):
    return (
        jnp.sum(storage_block * center[None], axis=1)
        + face_flux(coupling, field_ext)
        + phase_well * center
    )


def shards(rock_class, well_mask, perm_table, poro_table, accum, mobility, right_side):
    classes = perm_table.shape[0]
    onehot = (rock_class[None] == jnp.arange(classes, dtype=jnp.int32)[:, None, None, None]).astype(
        jnp.float32
    )
    looked = jnp.einsum(
        "tk,kxyz->txyz",
        jnp.stack([perm_table, poro_table]),
        onehot,
        precision=lax.Precision.HIGHEST,
    )
    permeability = looked[0]
    porosity = looked[1]
    storage_block = porosity * accum
    well_term = WELL_FACTOR * permeability * well_mask.astype(jnp.float32)
    phase_well = well_term * mobility
    stacked = jnp.concatenate([permeability[None], mobility], axis=0)
    rimmed = padded_2(stacked, (("gx", 1), ("gy", 2)), 1)
    coupling = couplings(rimmed[0], rimmed[0], rimmed[1:4])
    inverse = invert_blocks(
        storage_block + identity_blocks() * (phase_diagonal(coupling) + phase_well)
    )
    summed = tuple((jnp.sum(member, axis=0) for member in coupling))
    storage = jnp.sum(storage_block, axis=(0, 1)) + well_term * jnp.sum(mobility, axis=0)

    def pressure_operator(pressure_field):
        padded = padded_2(pressure_field, (("gx", 0), ("gy", 1)), 1)
        return storage * pressure_field + face_flux(summed, padded)

    source = jnp.sum(right_side, axis=0)
    solution = jnp.zeros_like(source)
    residual = source
    applied = pressure_operator(residual)
    direction = jnp.zeros_like(source)
    carried = jnp.zeros_like(source)
    bent = jnp.zeros_like(source)
    norm_old = None
    step_old = None
    for iteration in range(ITERS):
        norm_now, curvature = lax.psum(
            (jnp.sum(residual * residual), jnp.sum(applied * residual)), ("gx", "gy")
        )
        if iteration + 1 < ITERS:
            images = pressure_operator(applied)
        if iteration == 0:
            mixing = 0.0
            step_size = norm_now / curvature
        else:
            mixing = norm_now / norm_old
            step_size = norm_now / (curvature - mixing * norm_now / step_old)
        if iteration + 1 < ITERS:
            bent = images + mixing * bent
        carried = applied + mixing * carried
        direction = residual + mixing * direction
        solution = solution + step_size * direction
        residual = residual - step_size * carried
        if iteration + 1 < ITERS:
            applied = applied - step_size * bent
        norm_old = norm_now
        step_old = step_size
    pressure_cycle = padded_2(solution, (("gx", 0), ("gy", 1)), 1)
    start_ext = jnp.broadcast_to(pressure_cycle[None], (3,) + pressure_cycle.shape)
    start_center = start_ext[:, 1:-1, 1:-1]
    defect = right_side - jacobian(storage_block, coupling, phase_well, start_center, start_ext)
    update = start_center + jnp.sum(inverse * defect[None], axis=1)
    update_cycle = padded_2(update, (("gx", 1), ("gy", 2)), 1)
    defect = right_side - jacobian(storage_block, coupling, phase_well, update, update_cycle)
    correction = update + jnp.sum(inverse * defect[None], axis=1)
    return (solution, correction)


def solution(mesh):
    return jax.shard_map(
        shards,
        mesh=mesh,
        in_specs=(
            P("gx", "gy", None),
            P("gx", "gy", None),
            P(),
            P(),
            P(None, None, "gx", "gy", None),
            P(None, "gx", "gy", None),
            P(None, "gx", "gy", None),
        ),
        out_specs=(P("gx", "gy", None), P(None, "gx", "gy", None)),
        check_vma=False,
    )
```

profile of v0, /device:TPU:12, one launch (start us, length us, event | category | flops | bytes accessed | tf_op | source)
XLA Modules:
  0.0 228.4 jit_solution(13850948903285792661)
XLA Ops:
  1.7 3.5 %collective-permute-start.5 = (f32[1,16,128]{2,1,0:T(8,128)S(1)}, f32[1,16,128]{2,1,0:T(8,128)S(1)}, u32[]{:S(2)}, u32[]{:S(2)}) collective-permute-start(f32[1,16,128]{2,1,0:T(8,128)S(1)} %get-tuple-element.60), channel_id=1, source_target_pairs={{0,8},{8,16},{16,24},{1,9},{9,17},{17,25},{2,10},{10,18},{18,26},{... | collective-permute-start | bytes 24584 | tf_op jit(solution)/shard_map/ppermute | solution.py:22
  5.2 2.4 %collective-permute-start.4 = (f32[1,16,128]{2,1,0:T(8,128)S(1)}, f32[1,16,128]{2,1,0:T(8,128)S(1)}, u32[]{:S(2)}, u32[]{:S(2)}) collective-permute-start(f32[1,16,128]{2,1,0:T(8,128)S(1)} %get-tuple-element.61), channel_id=1, source_target_pairs={{8,0},{16,8},{24,16},{9,1},{17,9},{25,17},{10,2},{18,10},{26,18},{... | collective-permute-start | bytes 24584 | tf_op jit(solution)/shard_map/ppermute | solution.py:23
  9.6 3.5 %collective-permute-start = (f32[4,1,16,128]{3,2,1,0:T(8,128)S(1)}, f32[4,1,16,128]{3,2,1,0:T(8,128)S(1)}, u32[]{:S(2)}, u32[]{:S(2)}) collective-permute-start(f32[4,1,16,128]{3,2,1,0:T(8,128)S(1)} %get-tuple-element.33), channel_id=1, source_target_pairs={{0,8},{8,16},{16,24},{1,9},{9,17},{17,25},{2,10},{10,18},{18,26},{... | collective-permute-start | bytes 98312 | tf_op jit(solution)/shard_map/ppermute | solution.py:22
  13.1 2.4 %collective-permute-start.1 = (f32[4,1,16,128]{3,2,1,0:T(8,128)S(1)}, f32[4,1,16,128]{3,2,1,0:T(8,128)S(1)}, u32[]{:S(2)}, u32[]{:S(2)}) collective-permute-start(f32[4,1,16,128]{3,2,1,0:T(8,128)S(1)} %get-tuple-element.34), channel_id=1, source_target_pairs={{8,0},{16,8},{24,16},{9,1},{17,9},{25,17},{10,2},{18,10},{26,18},{... | collective-permute-start | bytes 98312 | tf_op jit(solution)/shard_map/ppermute | solution.py:23
  15.5 3.4 %collective-permute-done.1 = f32[4,1,16,128]{3,2,1,0:T(8,128)S(1)} collective-permute-done((f32[4,1,16,128]{3,2,1,0:T(8,128)S(1)}, f32[4,1,16,128]{3,2,1,0:T(8,128)S(1)}, u32[]{:S(2)}, u32[]{:S(2)}) %collective-permute-start.1) | collective-permute-done | bytes 32800 | tf_op jit(solution)/shard_map/ppermute | solution.py:23
  18.9 1.9 collective-permute-start.2
  20.8 4.5 %collective-permute-start.3 = (f32[4,10,1,128]{3,2,1,0:T(1,128)S(1)}, f32[4,10,1,128]{3,2,1,0:T(1,128)S(1)}, u32[]{:S(2)}, u32[]{:S(2)}) collective-permute-start(f32[4,10,1,128]{3,2,1,0:T(1,128)S(1)} %get-tuple-element.32), channel_id=1, source_target_pairs={{1,0},{2,1},{3,2},{4,3},{5,4},{6,5},{7,6},{9,8},{10,9},{11,10},{12... | collective-permute-start | bytes 61448 | tf_op jit(solution)/shard_map/ppermute | solution.py:23
  27.4 2.4 %collective-permute-start.7 = (f32[10,1,128]{2,1,0:T(1,128)S(1)}, f32[10,1,128]{2,1,0:T(1,128)S(1)}, u32[]{:S(2)}, u32[]{:S(2)}) collective-permute-start(f32[10,1,128]{2,1,0:T(1,128)S(1)} %get-tuple-element.51), channel_id=1, source_target_pairs={{0,1},{1,2},{2,3},{3,4},{4,5},{5,6},{6,7},{8,9},{9,10},{10,11},{11... | collective-permute-start | bytes 15368 | tf_op jit(solution)/shard_map/ppermute | solution.py:22
  30.5 2.7 %collective-permute-done.7 = f32[10,1,128]{2,1,0:T(1,128)S(1)} collective-permute-done((f32[10,1,128]{2,1,0:T(1,128)S(1)}, f32[10,1,128]{2,1,0:T(1,128)S(1)}, u32[]{:S(2)}, u32[]{:S(2)}) %collective-permute-start.7) | collective-permute-done | bytes 5152 | tf_op jit(solution)/shard_map/ppermute | solution.py:22
  33.9 3.5 %collective-permute-start.9 = (f32[1,16,128]{2,1,0:T(8,128)S(1)}, f32[1,16,128]{2,1,0:T(8,128)S(1)}, u32[]{:S(2)}, u32[]{:S(2)}) collective-permute-start(f32[1,16,128]{2,1,0:T(8,128)S(1)} %get-tuple-element.58), channel_id=1, source_target_pairs={{0,8},{8,16},{16,24},{1,9},{9,17},{17,25},{2,10},{10,18},{18,26},{... | collective-permute-start | bytes 24584 | tf_op jit(solution)/shard_map/ppermute | solution.py:22
  37.4 2.4 %collective-permute-start.8 = (f32[1,16,128]{2,1,0:T(8,128)S(1)}, f32[1,16,128]{2,1,0:T(8,128)S(1)}, u32[]{:S(2)}, u32[]{:S(2)}) collective-permute-start(f32[1,16,128]{2,1,0:T(8,128)S(1)} %get-tuple-element.59), channel_id=1, source_target_pairs={{8,0},{16,8},{24,16},{9,1},{17,9},{25,17},{10,2},{18,10},{26,18},{... | collective-permute-start | bytes 24584 | tf_op jit(solution)/shard_map/ppermute | solution.py:23
  39.8 3.2 %collective-permute-done.8 = f32[1,16,128]{2,1,0:T(8,128)S(1)} collective-permute-done((f32[1,16,128]{2,1,0:T(8,128)S(1)}, f32[1,16,128]{2,1,0:T(8,128)S(1)}, u32[]{:S(2)}, u32[]{:S(2)}) %collective-permute-start.8) | collective-permute-done | bytes 8224 | tf_op jit(solution)/shard_map/ppermute | solution.py:23
  44.9 2.4 %collective-permute-start.11 = (f32[10,1,128]{2,1,0:T(1,128)S(1)}, f32[10,1,128]{2,1,0:T(1,128)S(1)}, u32[]{:S(2)}, u32[]{:S(2)}) collective-permute-start(f32[10,1,128]{2,1,0:T(1,128)S(1)} %get-tuple-element.49), channel_id=1, source_target_pairs={{0,1},{1,2},{2,3},{3,4},{4,5},{5,6},{6,7},{8,9},{9,10},{10,11},{11... | collective-permute-start | bytes 15368 | tf_op jit(solution)/shard_map/ppermute | solution.py:22
  47.3 40.0 %all-reduce.14 = (f32[]{:T(128)}, f32[]{:T(128)}) all-reduce(f32[]{:T(128)} %get-tuple-element.5, f32[]{:T(128)} %get-tuple-element.4), channel_id=1, replica_groups=mesh['gx'=4,'gy'=8] {'gx','gy'}, use_global_device_ids=true, to_apply=%region_2.0 | all-reduce | flops 2 | bytes 16 | tf_op jit(solution)/shard_map/psum | solution.py:164
  88.8 2.6 %collective-permute-start.13 = (f32[1,16,128]{2,1,0:T(8,128)S(1)}, f32[1,16,128]{2,1,0:T(8,128)S(1)}, u32[]{:S(2)}, u32[]{:S(2)}) collective-permute-start(f32[1,16,128]{2,1,0:T(8,128)S(1)} %get-tuple-element.56), channel_id=1, source_target_pairs={{0,8},{8,16},{16,24},{1,9},{9,17},{17,25},{2,10},{10,18},{18,26},{... | collective-permute-start | bytes 24584 | tf_op jit(solution)/shard_map/ppermute | solution.py:22
  91.4 3.3 %collective-permute-start.12 = (f32[1,16,128]{2,1,0:T(8,128)S(1)}, f32[1,16,128]{2,1,0:T(8,128)S(1)}, u32[]{:S(2)}, u32[]{:S(2)}) collective-permute-start(f32[1,16,128]{2,1,0:T(8,128)S(1)} %get-tuple-element.57), channel_id=1, source_target_pairs={{8,0},{16,8},{24,16},{9,1},{17,9},{25,17},{10,2},{18,10},{26,18},{... | collective-permute-start | bytes 24584 | tf_op jit(solution)/shard_map/ppermute | solution.py:23
  95.3 40.2 %all-reduce.13 = (f32[]{:T(128)}, f32[]{:T(128)}) all-reduce(f32[]{:T(128)} %get-tuple-element.3, f32[]{:T(128)} %get-tuple-element.2), channel_id=1, replica_groups=mesh['gx'=4,'gy'=8] {'gx','gy'}, use_global_device_ids=true, to_apply=%region_11.0 | all-reduce | flops 2 | bytes 16 | tf_op jit(solution)/shard_map/psum | solution.py:164
  140.2 1.9 collective-permute-start.14
  142.1 2.4 %collective-permute-start.15 = (f32[10,1,128]{2,1,0:T(1,128)S(1)}, f32[10,1,128]{2,1,0:T(1,128)S(1)}, u32[]{:S(2)}, u32[]{:S(2)}) collective-permute-start(f32[10,1,128]{2,1,0:T(1,128)S(1)} %get-tuple-element.47), channel_id=1, source_target_pairs={{0,1},{1,2},{2,3},{3,4},{4,5},{5,6},{6,7},{8,9},{9,10},{10,11},{11... | collective-permute-start | bytes 15368 | tf_op jit(solution)/shard_map/ppermute | solution.py:22
  145.2 2.8 %collective-permute-done.15 = f32[10,1,128]{2,1,0:T(1,128)S(1)} collective-permute-done((f32[10,1,128]{2,1,0:T(1,128)S(1)}, f32[10,1,128]{2,1,0:T(1,128)S(1)}, u32[]{:S(2)}, u32[]{:S(2)}) %collective-permute-start.15) | collective-permute-done | bytes 5152 | tf_op jit(solution)/shard_map/ppermute | solution.py:22
  148.8 39.8 %all-reduce.12 = (f32[]{:T(128)}, f32[]{:T(128)}) all-reduce(f32[]{:T(128)} %multiply_reduce_fusion.5, f32[]{:T(128)} %fusion.100), channel_id=1, replica_groups=mesh['gx'=4,'gy'=8] {'gx','gy'}, use_global_device_ids=true, to_apply=%region_15.0 | all-reduce | flops 2 | bytes 16 | tf_op jit(solution)/shard_map/psum | solution.py:164
  192.9 2.6 %collective-permute-start.17 = (f32[1,16,128]{2,1,0:T(8,128)S(1)}, f32[1,16,128]{2,1,0:T(8,128)S(1)}, u32[]{:S(2)}, u32[]{:S(2)}) collective-permute-start(f32[1,16,128]{2,1,0:T(8,128)S(1)} %get-tuple-element.54), channel_id=1, source_target_pairs={{0,8},{8,16},{16,24},{1,9},{9,17},{17,25},{2,10},{10,18},{18,26},{... | collective-permute-start | bytes 24584 | tf_op jit(solution)/shard_map/ppermute | solution.py:22
  195.5 3.3 %collective-permute-start.16 = (f32[1,16,128]{2,1,0:T(8,128)S(1)}, f32[1,16,128]{2,1,0:T(8,128)S(1)}, u32[]{:S(2)}, u32[]{:S(2)}) collective-permute-start(f32[1,16,128]{2,1,0:T(8,128)S(1)} %get-tuple-element.55), channel_id=1, source_target_pairs={{8,0},{16,8},{24,16},{9,1},{17,9},{25,17},{10,2},{18,10},{26,18},{... | collective-permute-start | bytes 24584 | tf_op jit(solution)/shard_map/ppermute | solution.py:23
  198.8 2.2 collective-permute-done.16
  201.0 1.9 collective-permute-start.18
  203.0 2.4 %collective-permute-start.19 = (f32[10,1,128]{2,1,0:T(1,128)S(1)}, f32[10,1,128]{2,1,0:T(1,128)S(1)}, u32[]{:S(2)}, u32[]{:S(2)}) collective-permute-start(f32[10,1,128]{2,1,0:T(1,128)S(1)} %get-tuple-element.45), channel_id=1, source_target_pairs={{0,1},{1,2},{2,3},{3,4},{4,5},{5,6},{6,7},{8,9},{9,10},{10,11},{11... | collective-permute-start | bytes 15368 | tf_op jit(solution)/shard_map/ppermute | solution.py:22
  205.4 3.4 %collective-permute-done.19 = f32[10,1,128]{2,1,0:T(1,128)S(1)} collective-permute-done((f32[10,1,128]{2,1,0:T(1,128)S(1)}, f32[10,1,128]{2,1,0:T(1,128)S(1)}, u32[]{:S(2)}, u32[]{:S(2)}) %collective-permute-start.19) | collective-permute-done | bytes 5152 | tf_op jit(solution)/shard_map/ppermute | solution.py:22
  210.2 3.5 %collective-permute-start.21 = (f32[3,1,16,128]{3,2,1,0:T(8,128)S(1)}, f32[3,1,16,128]{3,2,1,0:T(8,128)S(1)}, u32[]{:S(2)}, u32[]{:S(2)}) collective-permute-start(f32[3,1,16,128]{3,2,1,0:T(8,128)S(1)} %get-tuple-element.37), channel_id=1, source_target_pairs={{0,8},{8,16},{16,24},{1,9},{9,17},{17,25},{2,10},{10,18},{18,26},{... | collective-permute-start | bytes 73736 | tf_op jit(solution)/shard_map/ppermute | solution.py:22
  213.7 2.3 %collective-permute-start.20 = (f32[3,1,16,128]{3,2,1,0:T(8,128)S(1)}, f32[3,1,16,128]{3,2,1,0:T(8,128)S(1)}, u32[]{:S(2)}, u32[]{:S(2)}) collective-permute-start(f32[3,1,16,128]{3,2,1,0:T(8,128)S(1)} %get-tuple-element.38), channel_id=1, source_target_pairs={{8,0},{16,8},{24,16},{9,1},{17,9},{25,17},{10,2},{18,10},{26,18},{... | collective-permute-start | bytes 73736 | tf_op jit(solution)/shard_map/ppermute | solution.py:23
  216.1 3.4 %collective-permute-done.20 = f32[3,1,16,128]{3,2,1,0:T(8,128)S(1)} collective-permute-done((f32[3,1,16,128]{3,2,1,0:T(8,128)S(1)}, f32[3,1,16,128]{3,2,1,0:T(8,128)S(1)}, u32[]{:S(2)}, u32[]{:S(2)}) %collective-permute-start.20) | collective-permute-done | bytes 24608 | tf_op jit(solution)/shard_map/ppermute | solution.py:23
  221.4 2.4 %collective-permute-start.23 = (f32[3,10,1,128]{3,2,1,0:T(1,128)S(1)}, f32[3,10,1,128]{3,2,1,0:T(1,128)S(1)}, u32[]{:S(2)}, u32[]{:S(2)}) collective-permute-start(f32[3,10,1,128]{3,2,1,0:T(1,128)S(1)} %get-tuple-element.36), channel_id=1, source_target_pairs={{0,1},{1,2},{2,3},{3,4},{4,5},{5,6},{6,7},{8,9},{9,10},{10,11},{11... | collective-permute-start | bytes 46088 | tf_op jit(solution)/shard_map/ppermute | solution.py:22
  223.9 3.5 %collective-permute-done.23 = f32[3,10,1,128]{3,2,1,0:T(1,128)S(1)} collective-permute-done((f32[3,10,1,128]{3,2,1,0:T(1,128)S(1)}, f32[3,10,1,128]{3,2,1,0:T(1,128)S(1)}, u32[]{:S(2)}, u32[]{:S(2)}) %collective-permute-start.23) | collective-permute-done | bytes 15392 | tf_op jit(solution)/shard_map/ppermute | solution.py:22
  (83 shorter events, 15.6 us)
Async XLA Ops:
  0.6 6.9 %copy-start.5 = (s32[8,16,128]{2,1,0:T(8,128)S(1)}, s32[8,16,128]{2,1,0:T(8,128)}, u32[]{:S(2)}) copy-start(s32[8,16,128]{2,1,0:T(8,128)} %param.7) | copy-start | bytes 196612
  0.6 14.8 %copy-start.1 = (f32[3,3,8,16,128]{4,3,2,1,0:T(8,128)S(1)}, f32[3,3,8,16,128]{4,3,2,1,0:T(8,128)}, u32[]{:S(2)}) copy-start(f32[3,3,8,16,128]{4,3,2,1,0:T(8,128)} %param.11) | copy-start | bytes 1769476
  1.7 23.7 %collective-permute-start.5 = (f32[1,16,128]{2,1,0:T(8,128)S(1)}, f32[1,16,128]{2,1,0:T(8,128)S(1)}, u32[]{:S(2)}, u32[]{:S(2)}) collective-permute-start(f32[1,16,128]{2,1,0:T(8,128)S(1)} %get-tuple-element.60), channel_id=1, source_target_pairs={{0,8},{8,16},{16,24},{1,9},{9,17},{17,25},{2,10},{10,18},{18,26},{... | collective-permute-start | bytes 24584 | tf_op jit(solution)/shard_map/ppermute | solution.py:22
  5.2 20.2 %collective-permute-start.4 = (f32[1,16,128]{2,1,0:T(8,128)S(1)}, f32[1,16,128]{2,1,0:T(8,128)S(1)}, u32[]{:S(2)}, u32[]{:S(2)}) collective-permute-start(f32[1,16,128]{2,1,0:T(8,128)S(1)} %get-tuple-element.61), channel_id=1, source_target_pairs={{8,0},{16,8},{24,16},{9,1},{17,9},{25,17},{10,2},{18,10},{26,18},{... | collective-permute-start | bytes 24584 | tf_op jit(solution)/shard_map/ppermute | solution.py:23
  8.6 0.9 copy-start
  9.6 5.9 %collective-permute-start = (f32[4,1,16,128]{3,2,1,0:T(8,128)S(1)}, f32[4,1,16,128]{3,2,1,0:T(8,128)S(1)}, u32[]{:S(2)}, u32[]{:S(2)}) collective-permute-start(f32[4,1,16,128]{3,2,1,0:T(8,128)S(1)} %get-tuple-element.33), channel_id=1, source_target_pairs={{0,8},{8,16},{16,24},{1,9},{9,17},{17,25},{2,10},{10,18},{18,26},{... | collective-permute-start | bytes 98312 | tf_op jit(solution)/shard_map/ppermute | solution.py:22
  13.1 5.8 %collective-permute-start.1 = (f32[4,1,16,128]{3,2,1,0:T(8,128)S(1)}, f32[4,1,16,128]{3,2,1,0:T(8,128)S(1)}, u32[]{:S(2)}, u32[]{:S(2)}) collective-permute-start(f32[4,1,16,128]{3,2,1,0:T(8,128)S(1)} %get-tuple-element.34), channel_id=1, source_target_pairs={{8,0},{16,8},{24,16},{9,1},{17,9},{25,17},{10,2},{18,10},{26,18},{... | collective-permute-start | bytes 98312 | tf_op jit(solution)/shard_map/ppermute | solution.py:23
  18.9 10.9 %collective-permute-start.2 = (f32[4,10,1,128]{3,2,1,0:T(1,128)S(1)}, f32[4,10,1,128]{3,2,1,0:T(1,128)S(1)}, u32[]{:S(2)}, u32[]{:S(2)}) collective-permute-start(f32[4,10,1,128]{3,2,1,0:T(1,128)S(1)} %get-tuple-element.31), channel_id=1, source_target_pairs={{0,1},{1,2},{2,3},{3,4},{4,5},{5,6},{6,7},{8,9},{9,10},{10,11},{11... | collective-permute-start | bytes 61448 | tf_op jit(solution)/shard_map/ppermute | solution.py:22
  20.8 8.9 %collective-permute-start.3 = (f32[4,10,1,128]{3,2,1,0:T(1,128)S(1)}, f32[4,10,1,128]{3,2,1,0:T(1,128)S(1)}, u32[]{:S(2)}, u32[]{:S(2)}) collective-permute-start(f32[4,10,1,128]{3,2,1,0:T(1,128)S(1)} %get-tuple-element.32), channel_id=1, source_target_pairs={{1,0},{2,1},{3,2},{4,3},{5,4},{6,5},{7,6},{9,8},{10,9},{11,10},{12... | collective-permute-start | bytes 61448 | tf_op jit(solution)/shard_map/ppermute | solution.py:23
  25.4 5.1 %collective-permute-start.6 = (f32[10,1,128]{2,1,0:T(1,128)S(1)}, f32[10,1,128]{2,1,0:T(1,128)S(1)}, u32[]{:S(2)}, u32[]{:S(2)}) collective-permute-start(f32[10,1,128]{2,1,0:T(1,128)S(1)} %get-tuple-element.50), channel_id=1, source_target_pairs={{1,0},{2,1},{3,2},{4,3},{5,4},{6,5},{7,6},{9,8},{10,9},{11,10},{12... | collective-permute-start | bytes 15368 | tf_op jit(solution)/shard_map/ppermute | solution.py:23
  27.4 5.8 %collective-permute-start.7 = (f32[10,1,128]{2,1,0:T(1,128)S(1)}, f32[10,1,128]{2,1,0:T(1,128)S(1)}, u32[]{:S(2)}, u32[]{:S(2)}) collective-permute-start(f32[10,1,128]{2,1,0:T(1,128)S(1)} %get-tuple-element.51), channel_id=1, source_target_pairs={{0,1},{1,2},{2,3},{3,4},{4,5},{5,6},{6,7},{8,9},{9,10},{10,11},{11... | collective-permute-start | bytes 15368 | tf_op jit(solution)/shard_map/ppermute | solution.py:22
  30.3 2.9 %copy-start.4 = (s32[8,16,128]{2,1,0:T(8,128)S(1)}, s32[8,16,128]{2,1,0:T(8,128)}, u32[]{:S(2)}) copy-start(s32[8,16,128]{2,1,0:T(8,128)} %param.8) | copy-start | bytes 196612
  33.9 5.8 %collective-permute-start.9 = (f32[1,16,128]{2,1,0:T(8,128)S(1)}, f32[1,16,128]{2,1,0:T(8,128)S(1)}, u32[]{:S(2)}, u32[]{:S(2)}) collective-permute-start(f32[1,16,128]{2,1,0:T(8,128)S(1)} %get-tuple-element.58), channel_id=1, source_target_pairs={{0,8},{8,16},{16,24},{1,9},{9,17},{17,25},{2,10},{10,18},{18,26},{... | collective-permute-start | bytes 24584 | tf_op jit(solution)/shard_map/ppermute | solution.py:22
  37.4 5.5 %collective-permute-start.8 = (f32[1,16,128]{2,1,0:T(8,128)S(1)}, f32[1,16,128]{2,1,0:T(8,128)S(1)}, u32[]{:S(2)}, u32[]{:S(2)}) collective-permute-start(f32[1,16,128]{2,1,0:T(8,128)S(1)} %get-tuple-element.59), channel_id=1, source_target_pairs={{8,0},{16,8},{24,16},{9,1},{17,9},{25,17},{10,2},{18,10},{26,18},{... | collective-permute-start | bytes 24584 | tf_op jit(solution)/shard_map/ppermute | solution.py:23
  43.0 45.6 %collective-permute-start.10 = (f32[10,1,128]{2,1,0:T(1,128)S(1)}, f32[10,1,128]{2,1,0:T(1,128)S(1)}, u32[]{:S(2)}, u32[]{:S(2)}) collective-permute-start(f32[10,1,128]{2,1,0:T(1,128)S(1)} %get-tuple-element.48), channel_id=1, source_target_pairs={{1,0},{2,1},{3,2},{4,3},{5,4},{6,5},{7,6},{9,8},{10,9},{11,10},{12... | collective-permute-start | bytes 15368 | tf_op jit(solution)/shard_map/ppermute | solution.py:23
  44.9 43.7 %collective-permute-start.11 = (f32[10,1,128]{2,1,0:T(1,128)S(1)}, f32[10,1,128]{2,1,0:T(1,128)S(1)}, u32[]{:S(2)}, u32[]{:S(2)}) collective-permute-start(f32[10,1,128]{2,1,0:T(1,128)S(1)} %get-tuple-element.49), channel_id=1, source_target_pairs={{0,1},{1,2},{2,3},{3,4},{4,5},{5,6},{6,7},{8,9},{9,10},{10,11},{11... | collective-permute-start | bytes 15368 | tf_op jit(solution)/shard_map/ppermute | solution.py:22
  88.8 51.4 %collective-permute-start.13 = (f32[1,16,128]{2,1,0:T(8,128)S(1)}, f32[1,16,128]{2,1,0:T(8,128)S(1)}, u32[]{:S(2)}, u32[]{:S(2)}) collective-permute-start(f32[1,16,128]{2,1,0:T(8,128)S(1)} %get-tuple-element.56), channel_id=1, source_target_pairs={{0,8},{8,16},{16,24},{1,9},{9,17},{17,25},{2,10},{10,18},{18,26},{... | collective-permute-start | bytes 24584 | tf_op jit(solution)/shard_map/ppermute | solution.py:22
  91.4 48.8 %collective-permute-start.12 = (f32[1,16,128]{2,1,0:T(8,128)S(1)}, f32[1,16,128]{2,1,0:T(8,128)S(1)}, u32[]{:S(2)}, u32[]{:S(2)}) collective-permute-start(f32[1,16,128]{2,1,0:T(8,128)S(1)} %get-tuple-element.57), channel_id=1, source_target_pairs={{8,0},{16,8},{24,16},{9,1},{17,9},{25,17},{10,2},{18,10},{26,18},{... | collective-permute-start | bytes 24584 | tf_op jit(solution)/shard_map/ppermute | solution.py:23
  140.2 5.0 %collective-permute-start.14 = (f32[10,1,128]{2,1,0:T(1,128)S(1)}, f32[10,1,128]{2,1,0:T(1,128)S(1)}, u32[]{:S(2)}, u32[]{:S(2)}) collective-permute-start(f32[10,1,128]{2,1,0:T(1,128)S(1)} %get-tuple-element.46), channel_id=1, source_target_pairs={{1,0},{2,1},{3,2},{4,3},{5,4},{6,5},{7,6},{9,8},{10,9},{11,10},{12... | collective-permute-start | bytes 15368 | tf_op jit(solution)/shard_map/ppermute | solution.py:23
  142.1 5.8 %collective-permute-start.15 = (f32[10,1,128]{2,1,0:T(1,128)S(1)}, f32[10,1,128]{2,1,0:T(1,128)S(1)}, u32[]{:S(2)}, u32[]{:S(2)}) collective-permute-start(f32[10,1,128]{2,1,0:T(1,128)S(1)} %get-tuple-element.47), channel_id=1, source_target_pairs={{0,1},{1,2},{2,3},{3,4},{4,5},{5,6},{6,7},{8,9},{9,10},{10,11},{11... | collective-permute-start | bytes 15368 | tf_op jit(solution)/shard_map/ppermute | solution.py:22
  192.6 35.1 %copy-start.2 = (f32[8,16,128]{2,1,0:T(8,128)}, f32[8,16,128]{2,1,0:T(8,128)S(1)}, u32[]{:S(2)}) copy-start(f32[8,16,128]{2,1,0:T(8,128)S(1)} %multiply_add_fusion.1) | copy-start | bytes 196612
  192.9 5.9 %collective-permute-start.17 = (f32[1,16,128]{2,1,0:T(8,128)S(1)}, f32[1,16,128]{2,1,0:T(8,128)S(1)}, u32[]{:S(2)}, u32[]{:S(2)}) collective-permute-start(f32[1,16,128]{2,1,0:T(8,128)S(1)} %get-tuple-element.54), channel_id=1, source_target_pairs={{0,8},{8,16},{16,24},{1,9},{9,17},{17,25},{2,10},{10,18},{18,26},{... | collective-permute-start | bytes 24584 | tf_op jit(solution)/shard_map/ppermute | solution.py:22
  195.5 5.5 %collective-permute-start.16 = (f32[1,16,128]{2,1,0:T(8,128)S(1)}, f32[1,16,128]{2,1,0:T(8,128)S(1)}, u32[]{:S(2)}, u32[]{:S(2)}) collective-permute-start(f32[1,16,128]{2,1,0:T(8,128)S(1)} %get-tuple-element.55), channel_id=1, source_target_pairs={{8,0},{16,8},{24,16},{9,1},{17,9},{25,17},{10,2},{18,10},{26,18},{... | collective-permute-start | bytes 24584 | tf_op jit(solution)/shard_map/ppermute | solution.py:23
  201.0 4.4 %collective-permute-start.18 = (f32[10,1,128]{2,1,0:T(1,128)S(1)}, f32[10,1,128]{2,1,0:T(1,128)S(1)}, u32[]{:S(2)}, u32[]{:S(2)}) collective-permute-start(f32[10,1,128]{2,1,0:T(1,128)S(1)} %get-tuple-element.44), channel_id=1, source_target_pairs={{1,0},{2,1},{3,2},{4,3},{5,4},{6,5},{7,6},{9,8},{10,9},{11,10},{12... | collective-permute-start | bytes 15368 | tf_op jit(solution)/shard_map/ppermute | solution.py:23
  203.0 5.8 %collective-permute-start.19 = (f32[10,1,128]{2,1,0:T(1,128)S(1)}, f32[10,1,128]{2,1,0:T(1,128)S(1)}, u32[]{:S(2)}, u32[]{:S(2)}) collective-permute-start(f32[10,1,128]{2,1,0:T(1,128)S(1)} %get-tuple-element.45), channel_id=1, source_target_pairs={{0,1},{1,2},{2,3},{3,4},{4,5},{5,6},{6,7},{8,9},{9,10},{10,11},{11... | collective-permute-start | bytes 15368 | tf_op jit(solution)/shard_map/ppermute | solution.py:22
  208.8 0.9 copy-start.3
  210.2 5.9 %collective-permute-start.21 = (f32[3,1,16,128]{3,2,1,0:T(8,128)S(1)}, f32[3,1,16,128]{3,2,1,0:T(8,128)S(1)}, u32[]{:S(2)}, u32[]{:S(2)}) collective-permute-start(f32[3,1,16,128]{3,2,1,0:T(8,128)S(1)} %get-tuple-element.37), channel_id=1, source_target_pairs={{0,8},{8,16},{16,24},{1,9},{9,17},{17,25},{2,10},{10,18},{18,26},{... | collective-permute-start | bytes 73736 | tf_op jit(solution)/shard_map/ppermute | solution.py:22
  213.7 5.7 %collective-permute-start.20 = (f32[3,1,16,128]{3,2,1,0:T(8,128)S(1)}, f32[3,1,16,128]{3,2,1,0:T(8,128)S(1)}, u32[]{:S(2)}, u32[]{:S(2)}) collective-permute-start(f32[3,1,16,128]{3,2,1,0:T(8,128)S(1)} %get-tuple-element.38), channel_id=1, source_target_pairs={{8,0},{16,8},{24,16},{9,1},{17,9},{25,17},{10,2},{18,10},{26,18},{... | collective-permute-start | bytes 73736 | tf_op jit(solution)/shard_map/ppermute | solution.py:23
  219.5 4.4 %collective-permute-start.22 = (f32[3,10,1,128]{3,2,1,0:T(1,128)S(1)}, f32[3,10,1,128]{3,2,1,0:T(1,128)S(1)}, u32[]{:S(2)}, u32[]{:S(2)}) collective-permute-start(f32[3,10,1,128]{3,2,1,0:T(1,128)S(1)} %get-tuple-element.35), channel_id=1, source_target_pairs={{1,0},{2,1},{3,2},{4,3},{5,4},{6,5},{7,6},{9,8},{10,9},{11,10},{12... | collective-permute-start | bytes 46088 | tf_op jit(solution)/shard_map/ppermute | solution.py:23
  221.4 5.9 %collective-permute-start.23 = (f32[3,10,1,128]{3,2,1,0:T(1,128)S(1)}, f32[3,10,1,128]{3,2,1,0:T(1,128)S(1)}, u32[]{:S(2)}, u32[]{:S(2)}) collective-permute-start(f32[3,10,1,128]{3,2,1,0:T(1,128)S(1)} %get-tuple-element.36), channel_id=1, source_target_pairs={{0,1},{1,2},{2,3},{3,4},{4,5},{5,6},{6,7},{8,9},{9,10},{10,11},{11... | collective-permute-start | bytes 46088 | tf_op jit(solution)/shard_map/ppermute | solution.py:22
where the time goes:
time: 230 us; the launch traced here: 228 us
  blocking collectives  120 us (52%)
  starting transfers between devices  63.1 us (27%)
  waiting for transfers between devices  24.4 us (11%)
  between operations  11.2 us (5%)
  other arithmetic  6.91 us (3%)
    psum x3, blocking collectives, shards(): lax.psum((jnp.sum(residual * residual), jnp.sum(applied * residual)), ('g...  120 us
    ppermute x12, starting transfers between devices, padded_2(): before = lax.ppermute(last, axis, up)  33 us
    ppermute x12, starting transfers between devices, padded_2(): after = lax.ppermute(initial, axis, down)  30.1 us
    ppermute x12, waiting for transfers between devices, padded_2(): before = lax.ppermute(last, axis, up)  12.3 us
    ppermute x12, waiting for transfers between devices, padded_2(): after = lax.ppermute(initial, axis, down)  12.1 us
  transfers between devices with their start and end apart: 24, of which 8 were waited for; matrix products, arithmetic and copies ran while one was open for 2% of the time, Pallas kernels for 0%

commit v1 on v0

v1 whole, which is shorter than its diff:
```python
import jax
import jax.numpy as jnp
from jax import lax
from jax.sharding import PartitionSpec as P

ITERS = 3
FACE_X = 1.0
FACE_Y = 1.0
FACE_Z = 2.0
WELL_FACTOR = 4.0
W = 4


def shift_both(up_payload, down_payload, axis):
    devices = lax.axis_size(axis)
    up = [(i, (i + 1) % devices) for i in range(devices - 1)]
    down = [(j, i) for i, j in up]
    return lax.ppermute(up_payload, axis, up), lax.ppermute(down_payload, axis, down)


def global_sum(values):
    axes = ("gx", "gy")
    total = 1
    for axis in axes:
        total *= lax.axis_size(axis)
    rows = jnp.broadcast_to(values[None], (total,) + values.shape)
    return jnp.sum(lax.all_to_all(rows, axes, 0, 0, tiled=True), axis=0)


def harmonic(left, right):
    return 2.0 * left * right / jnp.maximum(left + right, 0.005)


def faces(perm, weight, scale_x=FACE_X, scale_y=FACE_Y, scale_z=FACE_Z):
    cross_x = 0.5 * scale_x * harmonic(perm[:-1], perm[1:]) * (weight[..., :-1, :, :] + weight[..., 1:, :, :])
    cross_y = 0.5 * scale_y * harmonic(perm[:, :-1], perm[:, 1:]) * (weight[..., :-1, :] + weight[..., 1:, :])
    vertical = 0.5 * scale_z * harmonic(perm[..., :-1], perm[..., 1:]) * (weight[..., :-1] + weight[..., 1:])
    closed = jnp.zeros(vertical.shape[:-1] + (1,), jnp.float32)
    return cross_x, cross_y, jnp.concatenate([closed, vertical, closed], axis=-1)


def flux(coupling, field):
    cross_x, cross_y, cross_z = coupling
    center = field[..., 1:-1, 1:-1, :]
    closed = jnp.zeros_like(center[..., :1])
    lifted = jnp.concatenate([closed, center, closed], axis=-1)
    inner_x = cross_x[..., :, 1:-1, :]
    inner_y = cross_y[..., 1:-1, :, :]
    inner_z = cross_z[..., 1:-1, 1:-1, :]
    totals = inner_x[..., 1:, :, :] * (center - field[..., 2:, 1:-1, :])
    totals = totals + inner_x[..., :-1, :, :] * (center - field[..., :-2, 1:-1, :])
    totals = totals + inner_y[..., :, 1:, :] * (center - field[..., 1:-1, 2:, :])
    totals = totals + inner_y[..., :, :-1, :] * (center - field[..., 1:-1, :-2, :])
    totals = totals + inner_z[..., 1:] * (center - lifted[..., 2:])
    totals = totals + inner_z[..., :-1] * (center - lifted[..., :-2])
    return totals


def diagonal(coupling):
    cross_x, cross_y, cross_z = coupling
    inner_x = cross_x[..., :, 1:-1, :]
    inner_y = cross_y[..., 1:-1, :, :]
    inner_z = cross_z[..., 1:-1, 1:-1, :]
    totals = inner_x[..., 1:, :, :] + inner_x[..., :-1, :, :]
    totals = totals + inner_y[..., :, 1:, :] + inner_y[..., :, :-1, :]
    return totals + inner_z[..., 1:] + inner_z[..., :-1]


def trim(coupling, count):
    if not count:
        return coupling
    cut = slice(count, -count)
    return tuple(member[..., cut, cut, :] for member in coupling)


def adjugate(blocks):
    def cofactor(row_index, column_index):
        next_row = (row_index + 1) % 3
        last_row = (row_index + 2) % 3
        next_col = (column_index + 1) % 3
        last_col = (column_index + 2) % 3
        return (
            blocks[next_row][next_col] * blocks[last_row][last_col]
            - blocks[next_row][last_col] * blocks[last_row][next_col]
        )

    return [[cofactor(column, row) for column in range(3)] for row in range(3)]


def inner(first, second, moments, offset):
    total = 0.0
    for i, a in enumerate(first):
        for j, b in enumerate(second):
            total = total + a * b * moments[i + j + offset]
    return total


def combination(moments):
    residual = [1.0]
    direction = [1.0]
    result = [0.0] * ITERS
    norm_now = moments[0]
    for iteration in range(ITERS):
        step_size = norm_now / inner(direction, direction, moments, 1)
        for i, d in enumerate(direction):
            result[i] = result[i] + step_size * d
        if iteration + 1 == ITERS:
            break
        residual = residual + [0.0]
        for i, d in enumerate(direction):
            residual[i + 1] = residual[i + 1] - step_size * d
        norm_next = inner(residual, residual, moments, 0)
        mixing = norm_next / norm_now
        direction = [r + mixing * d for r, d in zip(residual, direction + [0.0])]
        norm_now = norm_next
    return result


def shards(rock_class, well_mask, perm_table, poro_table, accum, mobility, right_side):
    classes = perm_table.shape[0]
    permeability = jnp.zeros(rock_class.shape, jnp.float32)
    porosity = jnp.zeros(rock_class.shape, jnp.float32)
    for k in range(classes):
        permeability = jnp.where(rock_class == k, perm_table[k], permeability)
        porosity = jnp.where(rock_class == k, poro_table[k], porosity)
    storage_block = porosity * accum
    well_term = WELL_FACTOR * permeability * well_mask.astype(jnp.float32)
    summed_mobility = jnp.sum(mobility, axis=0)
    storage = jnp.sum(storage_block, axis=(0, 1)) + well_term * summed_mobility
    source = jnp.sum(right_side, axis=0)

    nx, ny, nz = source.shape
    wide = jnp.stack([source, permeability, summed_mobility, storage])
    near = jnp.concatenate([storage_block.reshape(9, nx, ny, nz), right_side, well_term[None]])
    groups = [(wide, W), (mobility, 2), (near, 1)]
    up = jnp.concatenate([g[:, nx - w :].reshape(-1, ny, nz) for g, w in groups])
    down = jnp.concatenate([g[:, :w].reshape(-1, ny, nz) for g, w in groups])
    before, after = shift_both(up, down, "gx")
    spread = []
    start = 0
    for g, w in groups:
        count = g.shape[0] * w
        first = before[start : start + count].reshape(g.shape[0], w, ny, nz)
        last = after[start : start + count].reshape(g.shape[0], w, ny, nz)
        spread.append(jnp.concatenate([first, g, last], axis=1))
        start += count
    up = jnp.concatenate([g[:, :, ny - w :].reshape(-1, nz) for g, (_, w) in zip(spread, groups)])
    down = jnp.concatenate([g[:, :, :w].reshape(-1, nz) for g, (_, w) in zip(spread, groups)])
    before, after = shift_both(up, down, "gy")
    full = []
    start = 0
    for g, (_, w) in zip(spread, groups):
        count = g.shape[0] * g.shape[1] * w
        shape = g.shape[:2] + (w, nz)
        first = before[start : start + count].reshape(shape)
        last = after[start : start + count].reshape(shape)
        full.append(jnp.concatenate([first, g, last], axis=2))
        start += count
    wide, mobile, near = full
    source_ext, perm_ext, sum_ext, storage_ext = wide

    summed = faces(perm_ext, sum_ext)

    def operate(field, depth):
        cut = W - depth + 1
        part = storage_ext[cut:-cut, cut:-cut]
        return part * field[1:-1, 1:-1] + flux(trim(summed, W - depth), field)

    basis = [source_ext]
    for depth in range(W, W - ITERS, -1):
        basis.append(operate(basis[-1], depth))

    def core(field):
        cut = (field.shape[0] - nx) // 2
        return field[cut:-cut, cut:-cut]

    locals_ = [core(b) for b in basis]
    moments = []
    for k in range(2 * ITERS):
        moments.append(jnp.sum(locals_[k // 2] * locals_[k - k // 2]))
    row = jnp.concatenate([jnp.stack(moments), jnp.zeros((nz - 2 * ITERS,), jnp.float32)])
    row = global_sum(row)
    weights = combination([row[k] for k in range(2 * ITERS)])

    pressure = 0.0
    for weight, b in zip(weights, basis[:ITERS]):
        cut = (b.shape[0] - nx) // 2 - 2
        pressure = pressure + weight * (b[cut:-cut, cut:-cut] if cut else b)

    perm_two = perm_ext[W - 2 : 2 - W, W - 2 : 2 - W]
    coupling = faces(perm_two, mobile)
    block = near[:9].reshape((3, 3) + near.shape[1:])
    right = near[9:12]
    phase_well = near[12] * mobile[:, 1:-1, 1:-1]
    spread_diagonal = diagonal(coupling) + phase_well
    blocks = [
        [block[p, q] + spread_diagonal[p] if p == q else block[p, q] for q in range(3)]
        for p in range(3)
    ]
    inverse = adjugate(blocks)
    determinant = sum(blocks[0][q] * inverse[q][0] for q in range(3))
    determinant = jnp.where(determinant == 0.0, 1.0, determinant)
    inverse = jnp.stack([jnp.stack(r) for r in inverse]) / determinant

    start_ext = jnp.broadcast_to(pressure[None], (3,) + pressure.shape)
    center = start_ext[:, 1:-1, 1:-1]
    image = jnp.sum(block * center[None], axis=1) + flux(coupling, start_ext) + phase_well * center
    update = center + jnp.sum(inverse * (right - image)[None], axis=1)
    cut = (slice(None), slice(1, -1), slice(1, -1))
    center = update[cut]
    image = (
        jnp.sum(block[:, :, 1:-1, 1:-1] * center[None], axis=1)
        + flux(trim(coupling, 1), update)
        + phase_well[cut] * center
    )
    correction = center + jnp.sum(
        inverse[:, :, 1:-1, 1:-1] * (right[cut] - image)[None], axis=1
    )
    return pressure[2:-2, 2:-2], correction


def solution(mesh):
    return jax.shard_map(
        shards,
        mesh=mesh,
        in_specs=(
            P("gx", "gy", None),
            P("gx", "gy", None),
            P(),
            P(),
            P(None, None, "gx", "gy", None),
            P(None, "gx", "gy", None),
            P(None, "gx", "gy", None),
        ),
        out_specs=(P("gx", "gy", None), P(None, "gx", "gy", None)),
        check_vma=False,
    )
```

time: 230 us -> 96.1 us (0.42)
  the two profiles are of different devices: /device:TPU:12 before, /device:TPU:0 now
where the time goes in v1:
time: 96.1 us; the launch traced here: 94.9 us
  other arithmetic  32.8 us (34%)
  starting transfers between devices  22.3 us (23%)
  local copies, waits for them, and re-layouts  17 us (18%)
  between operations  14.2 us (15%)
  waiting for transfers between devices  8.45 us (9%)
    select_n x1, other arithmetic, shards(): porosity = jnp.where(rock_class == k, poro_table[k], porosity)  11 us
    all_to_all x1, starting transfers between devices, global_sum(): return jnp.sum(lax.all_to_all(rows, axes, 0, 0, tiled=True), axis=0)  11 us
    another operation x2, other arithmetic, shards(): wide = jnp.stack([source, permeability, summed_mobility, storage])  10.2 us
    ppermute x2, starting transfers between devices, shift_both(): lax.ppermute(up_payload, axis, up)  8.78 us
    ppermute x2, waiting for transfers between devices, shift_both(): lax.ppermute(down_payload, axis, down)  4.7 us
    concatenate x1, local copies, waits for them, and re-layouts, shards(): jnp.concatenate([jnp.stack(moments), jnp.zeros((nz - 2 * ITERS,), jnp.flo...  3.75 us
    unnamed x54, local copies, waits for them, and re-layouts  3.33 us
    ppermute x2, starting transfers between devices, shift_both(): lax.ppermute(down_payload, axis, down)  2.58 us
  transfers between devices with their start and end apart: 5, of which 4 were waited for; matrix products, arithmetic and copies ran while one was open for 5% of the time, Pallas kernels for 0%

profile of v1, /device:TPU:0, one launch (start us, length us, event | category | flops | bytes accessed | tf_op | source)
XLA Modules:
  0.0 94.9 jit_solution(2069996665766408204)
XLA Ops:
  0.6 2.0 %fusion.94 = (f32[1]{0:T(128)}, f32[1]{0:T(128)}, f32[1]{0:T(128)}, f32[1]{0:T(128)}, f32[1]{0:T(128)}, /*index=5*/f32[1]{0:T(128)}, f32[1]{0:T(128)}, f32[1]{0:...) fusion(f32[16]{0:T(128)} %param.10), kind=kLoop, calls=%fused_computation.247 | loop fusion | bytes 128 | tf_op jit(solution)/shard_map/slice | solution.py:125
  2.6 0.8 fusion.91
  3.4 1.0 %reduce_sum.127 = f32[8,16,128]{2,1,0:T(8,128)S(1)} reduce(f32[3,8,16,128]{3,2,1,0:T(8,128)} %param.12, f32[]{:T(128)} %constant.22.clone.1), dimensions={0}, to_apply=%region_1.2 | reduce | flops 32768 | bytes 262148 | tf_op jit(solution)/shard_map/reduce_sum | solution.py:128
  4.4 2.0 %fusion.93 = (f32[1]{0:T(128)}, f32[1]{0:T(128)}, f32[1]{0:T(128)}, f32[1]{0:T(128)}, f32[1]{0:T(128)}, /*index=5*/f32[1]{0:T(128)}, f32[1]{0:T(128)}, f32[1]{0:...) fusion(f32[16]{0:T(128)} %param.9), kind=kLoop, calls=%fused_computation.246 | loop fusion | bytes 128 | tf_op jit(solution)/shard_map/slice | solution.py:124
  6.4 11.0 %select_select_fusion = (f32[8,16,128]{2,1,0:T(8,128)S(1)}, pred[8,16,128]{2,1,0:T(8,128)(4,1)S(1)}, pred[8,16,128]{2,1,0:T(8,128)(4,1)S(1)}, pred[8,16,128]{2,1...) fusion(f32[]{:T(128)} %bitcast.34, f32[]{:T(128)} %bitcast.33, ...), kind=kLoop, calls=%fused_computation.218 | loop fusion | flops 524288 | bytes 393280 | tf_op jit(solution)/shard_map/jit(_where)/select_n | solution.py:125
  17.5 10.2 %add_bitcast_fusion = (f32[1,8,16,128]{3,2,1,0:T(8,128)S(1)}, f32[8,16,128]{2,1,0:T(8,128)S(1)}) fusion(f32[8,16,128]{2,1,0:T(8,128)S(1)} %get-tuple-element.23, f32[8,16,128]{2,1,0:T(8,128)S(1)} %reduce_sum.127, s32[8,16,128]{2,1,0:T(8,128)S(1)} %copy-done.24, pred[8,16,128]{2,1,0:T(8,128)(4,1)S(1)} %get-tuple-element.41, ...), kind=kLoop, calls=%fused_computation.216 | loop fusion | flops 344064 | bytes 589888 | tf_op jit(solution)/shard_map/stack | solution.py:133
  28.0 1.3 %collective-permute-start.1 = (f32[35,16,128]{2,1,0:T(8,128)S(1)}, f32[35,16,128]{2,1,0:T(8,128)S(1)}, u32[]{:S(2)}, u32[]{:S(2)}) collective-permute-start(f32[35,16,128]{2,1,0:T(8,128)S(1)} %pad_maximum_fusion.5), channel_id=1, source_target_pairs={{8,0},{16,8},{24,16},{9,1},{17,9},{25,17},{10,2},{18,10},{26,18},{... | collective-permute-start | bytes 860168 | tf_op jit(solution)/shard_map/ppermute | solution.py:18
  29.4 5.7 %collective-permute-start = (f32[35,16,128]{2,1,0:T(8,128)S(1)}, f32[35,16,128]{2,1,0:T(8,128)S(1)}, u32[]{:S(2)}, u32[]{:S(2)}) collective-permute-start(f32[35,16,128]{2,1,0:T(8,128)S(1)} %pad_maximum_fusion.4), channel_id=1, source_target_pairs={{0,8},{8,16},{16,24},{1,9},{9,17},{17,25},{2,10},{10,18},{18,26},{... | collective-permute-start | bytes 860168 | tf_op jit(solution)/shard_map/ppermute | solution.py:18
  35.1 4.7 %collective-permute-done.1 = f32[35,16,128]{2,1,0:T(8,128)S(1)} collective-permute-done((f32[35,16,128]{2,1,0:T(8,128)S(1)}, f32[35,16,128]{2,1,0:T(8,128)S(1)}, u32[]{:S(2)}, u32[]{:S(2)}) %collective-permute-start.1) | collective-permute-done | bytes 286752 | tf_op jit(solution)/shard_map/ppermute | solution.py:18
  39.8 1.3 %collective-permute-done = f32[35,16,128]{2,1,0:T(8,128)S(1)} collective-permute-done((f32[35,16,128]{2,1,0:T(8,128)S(1)}, f32[35,16,128]{2,1,0:T(8,128)S(1)}, u32[]{:S(2)}, u32[]{:S(2)}) %collective-permute-start) | collective-permute-done | bytes 286752 | tf_op jit(solution)/shard_map/ppermute | solution.py:18
  42.4 1.3 %collective-permute-start.3 = (f32[458,128]{1,0:T(8,128)S(1)}, f32[458,128]{1,0:T(8,128)S(1)}, u32[]{:S(2)}, u32[]{:S(2)}) collective-permute-start(f32[458,128]{1,0:T(8,128)S(1)} %pad_maximum_fusion.8), channel_id=1, source_target_pairs={{1,0},{2,1},{3,2},{4,3},{5,4},{6,5},{7,6},{9,8},{10,9},{11,10},{12... | collective-permute-start | bytes 703496 | tf_op jit(solution)/shard_map/ppermute | solution.py:18
  43.7 3.0 %collective-permute-start.2 = (f32[458,128]{1,0:T(8,128)S(1)}, f32[458,128]{1,0:T(8,128)S(1)}, u32[]{:S(2)}, u32[]{:S(2)}) collective-permute-start(f32[458,128]{1,0:T(8,128)S(1)} %pad_maximum_fusion.7), channel_id=1, source_target_pairs={{0,1},{1,2},{2,3},{3,4},{4,5},{5,6},{6,7},{8,9},{9,10},{10,11},{11... | collective-permute-start | bytes 703496 | tf_op jit(solution)/shard_map/ppermute | solution.py:18
  46.8 1.1 %collective-permute-done.2 = f32[458,128]{1,0:T(8,128)S(1)} collective-permute-done((f32[458,128]{1,0:T(8,128)S(1)}, f32[458,128]{1,0:T(8,128)S(1)}, u32[]{:S(2)}, u32[]{:S(2)}) %collective-permute-start.2) | collective-permute-done | bytes 234528 | tf_op jit(solution)/shard_map/ppermute | solution.py:18
  49.0 0.7 divide_multiply_fusion.1
  49.7 0.8 maximum_divide_fusion.1
  51.7 0.8 fusion.82
  52.5 3.8 %concatenate.108 = f32[128]{0:T(128)S(1)} concatenate(f32[1]{0:T(128)} %bitcast.57, f32[1]{0:T(128)} %bitcast.64, f32[1]{0:T(128)} %bitcast.65, f32[1]{0:T(128)} %bitcast.66, f32[1]{0:T(128)} %bitcast.67, f32[1]{0:T(128)} %bitcast.68, f32[122]{0:T(128)S(1)} %broadcast_in_dim.176), dimensions={0} | concatenate | bytes 1024 | tf_op jit(solution)/shard_map/concatenate | solution.py:181
  56.3 0.6 broadcast_in_dim.177
  56.9 11.0 %all-to-all-start = ((f32[32,1,128]{2,1,0:T(1,128)}), f32[32,1,128]{2,1,0:T(1,128)}, u32[]{:S(2)}, u32[]{:S(2)}) async-start(f32[32,1,128]{2,1,0:T(1,128)} %broadcast_in_dim.177), calls=%async_computation | async-start | bytes 32768 | tf_op jit(solution)/shard_map/all_to_all | solution.py:27
  67.9 0.9 slice.917
  68.8 0.9 slice.916
  69.8 0.8 slice.922
  70.8 0.7 copy-done.18
  71.7 0.9 fusion.2
  72.9 0.7 maximum_bitcast_fusion.3
  73.7 1.4 %all-to-all-done = f32[32,1,128]{2,1,0:T(1,128)} async-done(((f32[32,1,128]{2,1,0:T(1,128)}), f32[32,1,128]{2,1,0:T(1,128)}, u32[]{:S(2)}, u32[]{:S(2)}) %all-to-all-start) | async-done | bytes 16416 | tf_op jit(solution)/shard_map/all_to_all | solution.py:27
  75.0 0.7 reduce_sum.135
  75.8 0.7 fusion.92
  89.3 1.0 %fusion.56 = f32[12,20,128]{2,1,0:T(8,128)S(1)} fusion(f32[16,24,128]{2,1,0:T(8,128)S(1)} %get-tuple-element.56, f32[12,20,128]{2,1,0:T(8,128)} %copy-done.2, f32[]{:T(128)S(6)} %mul.689, f32[]{:T(128)S(6)} %add.379, f32[]{:T(128)S(6)} %add.378, f32[14,22,128]{2,1,0:T(8,128)S(1)} %fusion.37), kind=kLoop, calls=%fused_computation.121 | loop fusion | flops 153600 | bytes 491532 | tf_op jit(solution)/shard_map/add | solution.py:188
  90.2 0.6 slice.914
  91.1 0.8 copy-done.1
  94.1 0.7 slice_add_fusion.7
  (120 shorter events, 6.7 us)
Async XLA Ops:
  0.6 16.8 %copy-start.17 = (f32[3,3,8,16,128]{4,3,2,1,0:T(8,128)S(1)}, f32[3,3,8,16,128]{4,3,2,1,0:T(8,128)}, u32[]{:S(2)}) copy-start(f32[3,3,8,16,128]{4,3,2,1,0:T(8,128)} %param.11) | copy-start | bytes 1769476
  3.4 14.1 %copy-start.24 = (s32[8,16,128]{2,1,0:T(8,128)S(1)}, s32[8,16,128]{2,1,0:T(8,128)}, u32[]{:S(2)}) copy-start(s32[8,16,128]{2,1,0:T(8,128)} %param.8) | copy-start | bytes 196612
  17.5 10.3 %copy-start = (f32[3,8,16,128]{3,2,1,0:T(8,128)S(1)}, f32[3,8,16,128]{3,2,1,0:T(8,128)}, u32[]{:S(2)}) copy-start(f32[3,8,16,128]{3,2,1,0:T(8,128)} %param.13) | copy-start | bytes 589828
  27.8 13.4 %copy-start.9 = (f32[1,8,16,128]{3,2,0,1:T(8,128)}, f32[1,8,16,128]{3,2,0,1:T(8,128)S(1)}, u32[]{:S(2)}) copy-start(f32[1,8,16,128]{3,2,0,1:T(8,128)S(1)} %fusion.87) | copy-start | bytes 196612
  28.0 11.8 %collective-permute-start.1 = (f32[35,16,128]{2,1,0:T(8,128)S(1)}, f32[35,16,128]{2,1,0:T(8,128)S(1)}, u32[]{:S(2)}, u32[]{:S(2)}) collective-permute-start(f32[35,16,128]{2,1,0:T(8,128)S(1)} %pad_maximum_fusion.5), channel_id=1, source_target_pairs={{8,0},{16,8},{24,16},{9,1},{17,9},{25,17},{10,2},{18,10},{26,18},{... | collective-permute-start | bytes 860168 | tf_op jit(solution)/shard_map/ppermute | solution.py:18
  29.4 12.8 %copy-start.7 = (f32[3,8,16,128]{3,2,1,0:T(8,128)S(1)}, f32[3,8,16,128]{3,2,1,0:T(8,128)}, u32[]{:S(2)}) copy-start(f32[3,8,16,128]{3,2,1,0:T(8,128)} %param.12) | copy-start | bytes 589828
  29.4 11.8 %collective-permute-start = (f32[35,16,128]{2,1,0:T(8,128)S(1)}, f32[35,16,128]{2,1,0:T(8,128)S(1)}, u32[]{:S(2)}, u32[]{:S(2)}) collective-permute-start(f32[35,16,128]{2,1,0:T(8,128)S(1)} %pad_maximum_fusion.4), channel_id=1, source_target_pairs={{0,8},{8,16},{16,24},{1,9},{9,17},{17,25},{2,10},{10,18},{18,26},{... | collective-permute-start | bytes 860168 | tf_op jit(solution)/shard_map/ppermute | solution.py:18
  39.8 33.0 %copy-start.3 = (f32[13,1,16,128]{3,2,1,0:T(8,128)}, f32[13,1,16,128]{3,2,1,0:T(8,128)S(1)}, u32[]{:S(2)}) copy-start(f32[13,1,16,128]{3,2,1,0:T(8,128)S(1)} %slice_bitcast_fusion.6) | copy-start | bytes 319492
  41.2 31.7 %copy-start.5 = (f32[13,1,16,128]{3,2,1,0:T(8,128)}, f32[13,1,16,128]{3,2,1,0:T(8,128)S(1)}, u32[]{:S(2)}) copy-start(f32[13,1,16,128]{3,2,1,0:T(8,128)S(1)} %slice_bitcast_fusion.7) | copy-start | bytes 319492
  41.6 0.7 copy-start.20
  42.4 4.4 %collective-permute-start.3 = (f32[458,128]{1,0:T(8,128)S(1)}, f32[458,128]{1,0:T(8,128)S(1)}, u32[]{:S(2)}, u32[]{:S(2)}) collective-permute-start(f32[458,128]{1,0:T(8,128)S(1)} %pad_maximum_fusion.8), channel_id=1, source_target_pairs={{1,0},{2,1},{3,2},{4,3},{5,4},{6,5},{7,6},{9,8},{10,9},{11,10},{12... | collective-permute-start | bytes 703496 | tf_op jit(solution)/shard_map/ppermute | solution.py:18
  43.7 4.1 %collective-permute-start.2 = (f32[458,128]{1,0:T(8,128)S(1)}, f32[458,128]{1,0:T(8,128)S(1)}, u32[]{:S(2)}, u32[]{:S(2)}) collective-permute-start(f32[458,128]{1,0:T(8,128)S(1)} %pad_maximum_fusion.7), channel_id=1, source_target_pairs={{0,1},{1,2},{2,3},{3,4},{4,5},{5,6},{6,7},{8,9},{9,10},{10,11},{11... | collective-permute-start | bytes 703496 | tf_op jit(solution)/shard_map/ppermute | solution.py:18
  46.8 1.1 %copy-start.25 = (f32[458,128]{1,0:T(8,128)}, f32[458,128]{1,0:T(8,128)S(1)}, u32[]{:S(2)}) copy-start(f32[458,128]{1,0:T(8,128)S(1)} %collective-permute-done.3) | copy-start | bytes 703492
  47.9 0.7 copy-start.26
  51.0 0.7 copy-start.2
  51.1 19.5 %copy-start.8 = (f32[3,8,16,128]{3,2,1,0:T(8,128)S(1)}, f32[3,8,16,128]{3,2,1,0:T(8,128)}, u32[]{:S(2)}) copy-start(f32[3,8,16,128]{3,2,1,0:T(8,128)} %param.12) | copy-start | bytes 589828
  51.1 19.5 %copy-start.21 = (f32[6,16,128]{2,1,0:T(8,128)S(1)}, f32[6,16,128]{2,1,0:T(8,128)}, u32[]{:S(2)}) copy-start(f32[6,16,128]{2,1,0:T(8,128)} %copy-done.20) | copy-start | bytes 147460
  51.1 19.5 %copy-start.23 = (f32[6,16,128]{2,1,0:T(8,128)S(1)}, f32[6,16,128]{2,1,0:T(8,128)}, u32[]{:S(2)}) copy-start(f32[6,16,128]{2,1,0:T(8,128)} %copy-done.22) | copy-start | bytes 147460
  51.3 19.4 %slice-start = ((f32[458,128]{1,0:T(8,128)}), f32[72,128]{1,0:T(8,128)S(1)}, s32[]{:S(2)}) async-start(f32[458,128]{1,0:T(8,128)} %copy-done.25), calls=%async_computation.1 | async-start | bytes 73728 | tf_op jit(solution)/shard_map/slice | solution.py:156
  56.9 18.1 %all-to-all-start = ((f32[32,1,128]{2,1,0:T(1,128)}), f32[32,1,128]{2,1,0:T(1,128)}, u32[]{:S(2)}, u32[]{:S(2)}) async-start(f32[32,1,128]{2,1,0:T(1,128)} %broadcast_in_dim.177), calls=%async_computation | async-start | bytes 32768 | tf_op jit(solution)/shard_map/all_to_all | solution.py:27
  68.8 4.1 %copy-start.12 = (f32[13,10,1,128]{3,2,1,0:T(1,128)}, f32[13,10,1,128]{3,2,1,0:T(1,128)S(1)}, u32[]{:S(2)}) copy-start(f32[13,10,1,128]{3,2,1,0:T(1,128)S(1)} %reshape.302) | copy-start | bytes 199684
  69.8 3.1 %copy-start.14 = (f32[13,10,1,128]{3,2,1,0:T(1,128)}, f32[13,10,1,128]{3,2,1,0:T(1,128)S(1)}, u32[]{:S(2)}) copy-start(f32[13,10,1,128]{3,2,1,0:T(1,128)S(1)} %reshape.301) | copy-start | bytes 199684
  70.7 0.9 copy-start.18
  70.7 0.9 copy-start.16
  71.6 1.0 %copy-start.10 = (f32[1,8,16,128]{3,2,0,1:T(8,128)S(1)}, f32[1,8,16,128]{3,2,0,1:T(8,128)}, u32[]{:S(2)}) copy-start(f32[1,8,16,128]{3,2,0,1:T(8,128)} %copy-done.9) | copy-start | bytes 196612
  90.9 1.0 %copy-start.1 = (f32[3,12,20,127]{3,2,1,0:T(8,128)S(1)}, f32[3,12,20,127]{3,2,1,0:T(8,128)}, u32[]{:S(2)}) copy-start(f32[3,12,20,127]{3,2,1,0:T(8,128)} %fusion.2) | copy-start | bytes 1097284
  90.9 1.0 %copy-start.4 = (f32[13,1,16,128]{3,2,1,0:T(8,128)S(1)}, f32[13,1,16,128]{3,2,1,0:T(8,128)}, u32[]{:S(2)}) copy-start(f32[13,1,16,128]{3,2,1,0:T(8,128)} %copy-done.3) | copy-start | bytes 319492
  90.9 1.1 %copy-start.6 = (f32[13,1,16,128]{3,2,1,0:T(8,128)S(1)}, f32[13,1,16,128]{3,2,1,0:T(8,128)}, u32[]{:S(2)}) copy-start(f32[13,1,16,128]{3,2,1,0:T(8,128)} %copy-done.5) | copy-start | bytes 319492
  91.0 1.1 %copy-start.11 = (f32[1,8,16,128]{3,2,0,1:T(8,128)S(1)}, f32[1,8,16,128]{3,2,0,1:T(8,128)}, u32[]{:S(2)}) copy-start(f32[1,8,16,128]{3,2,0,1:T(8,128)} %copy-done.9) | copy-start | bytes 196612
  91.0 1.1 %copy-start.13 = (f32[13,10,1,128]{3,2,1,0:T(1,128)S(1)}, f32[13,10,1,128]{3,2,1,0:T(1,128)}, u32[]{:S(2)}) copy-start(f32[13,10,1,128]{3,2,1,0:T(1,128)} %copy-done.12) | copy-start | bytes 199684
  91.0 1.1 %copy-start.15 = (f32[13,10,1,128]{3,2,1,0:T(1,128)S(1)}, f32[13,10,1,128]{3,2,1,0:T(1,128)}, u32[]{:S(2)}) copy-start(f32[13,10,1,128]{3,2,1,0:T(1,128)} %copy-done.14) | copy-start | bytes 199684
  91.0 1.1 %copy-start.19 = (f32[10,18,128]{2,1,0:T(8,128)S(1)}, f32[10,18,128]{2,1,0:T(8,128)}, u32[]{:S(2)}) copy-start(f32[10,18,128]{2,1,0:T(8,128)} %maximum_bitcast_fusion.3) | copy-start | bytes 276484
  (1 other events, 0.6 us)

commit v2 on v0

v2 whole, which is shorter than its diff:
```python
import jax
import jax.numpy as jnp
from jax import lax
from jax.experimental import pallas as pl
from jax.experimental.pallas import tpu as pltpu
from jax.sharding import PartitionSpec as P

ITERS = 3
FACE = (1.0, 1.0, 2.0)
WELL_FACTOR = 4.0
PERM_FLOOR = 0.005
W = 4
MOMENTS = 2 * ITERS
LOW = 8
STOP = 1e-12
LANES = 128
SUB = 8

VMEM = pl.BlockSpec(memory_space=pltpu.VMEM)
SMEM = pl.BlockSpec(memory_space=pltpu.SMEM)


def call(kernel, name, shapes, *operands, specs=None, scratch=()):
    out = [jax.ShapeDtypeStruct(shape, jnp.float32) for shape in shapes]
    return pl.pallas_call(
        kernel,
        name=name,
        out_shape=out,
        in_specs=specs or [VMEM] * len(operands),
        out_specs=[VMEM] * len(out),
        scratch_shapes=list(scratch),
    )(*operands)


class Grid:
    def __init__(self, nx, ny):
        self.nx, self.ny = nx, ny
        self.rows = nx * ny
        self.pitch = ny + 2 * W
        self.planes = nx + 2 * W
        self.total = (self.planes + 2) * self.pitch + SUB

    def at(self, x, y):
        return (x + W + 1) * self.pitch + y + W

    def chunks(self, depth):
        for x in range(-depth, self.nx + depth):
            for j in range(self.pitch // SUB):
                yield self.at(x, -W) + j * SUB

    def core(self):
        for x in range(self.nx):
            for j in range(self.ny // SUB):
                yield x * self.ny + j * SUB, self.at(x, j * SUB)


def rows(ref, start, count=SUB):
    return ref[pl.ds(start, count), :]


def harmonic(left, right):
    return left * right / jnp.maximum(left + right, PERM_FLOOR)


def ahead(value):
    return pltpu.roll(value, LANES - 1, 1)


def behind(value):
    return pltpu.roll(value, 1, 1)


def open_face():
    lane = lax.broadcasted_iota(jnp.int32, (SUB, LANES), 1)
    return jnp.where(lane == LANES - 1, 0.0, 1.0)


def two_sum(a, b):
    total = a + b
    part = total - a
    return total, (a - (total - part)) + (b - part)


def split(a):
    scaled = a * 4097.0
    high = scaled - (scaled - a)
    return high, a - high


def two_prod(a, b, a_parts=None, b_parts=None):
    a_high, a_low = a_parts or split(a)
    b_high, b_low = b_parts or split(b)
    product = a * b
    return product, ((a_high * b_high - product) + a_high * b_low + a_low * b_high) + a_low * b_low


def pair_add(a, b):
    total, error = two_sum(a[0], b[0])
    error = error + (a[1] + b[1])
    high = total + error
    return high, error - (high - total)


def pair_mul(a, b):
    product, error = two_prod(a[0], b[0])
    error = error + (a[0] * b[1] + a[1] * b[0])
    high = product + error
    return high, error - (high - product)


def pair_tree(terms):
    terms = list(terms)
    while len(terms) > 1:
        joined = [pair_add(a, b) for a, b in zip(terms[::2], terms[1::2])]
        terms = joined + terms[len(terms) - len(terms) % 2 :]
    return terms[0]


def squares(poly):
    out = []
    for k in range(2 * len(poly) - 1):
        terms = []
        for i in range(max(0, k - len(poly) + 1), k // 2 + 1):
            high, low = two_prod(poly[i], poly[k - i])
            scale = 1.0 if 2 * i == k else 2.0
            terms.append((scale * high, scale * low))
        out.append(pair_tree(terms))
    return out


def norm(poly, moments, offset):
    return pair_tree(
        pair_mul(s, moments[k + offset]) for k, s in enumerate(squares(poly))
    )[0]


def combination(moments):
    one = jnp.ones_like(moments[0][0])
    zero = jnp.zeros_like(one)
    first = moments[0][0]
    residual, direction = [one], [one]
    result = [zero] * ITERS
    norm_now = first
    for iteration in range(ITERS):
        curvature = norm(direction, moments, 1)
        step = norm_now / curvature
        if iteration:
            step = jnp.where((norm_now > STOP * first) & (curvature > 0.0), step, 0.0)
        result = [r + step * d for r, d in zip(result, direction)] + result[len(direction) :]
        if iteration + 1 == ITERS:
            break
        residual = residual + [zero]
        residual = [residual[0]] + [r - step * d for r, d in zip(residual[1:], direction)]
        norm_next = norm(residual, moments, 0)
        mixing = norm_next / norm_now
        if iteration:
            mixing = jnp.where(norm_now > STOP * first, mixing, 0.0)
        direction = [r + mixing * d for r, d in zip(residual, direction + [zero])]
        norm_now = norm_next
    return result


def prepare(grid, classes):
    nx, ny = grid.nx, grid.ny

    def kernel(perm_table, poro_table, rock, mask, accum, mobility, right, wide, near, a_up, a_down, b_up, b_down):
        for r in range(0, grid.rows, SUB):
            kind = rows(rock, r)
            perm = jnp.zeros((SUB, LANES), jnp.float32)
            poro = perm
            for k in range(classes):
                hit = kind == k
                perm = jnp.where(hit, perm_table[k], perm)
                poro = jnp.where(hit, poro_table[k], poro)
            well = (WELL_FACTOR * perm) * rows(mask, r).astype(jnp.float32)
            summed = rows(mobility.at[0], r) + rows(mobility.at[1], r) + rows(mobility.at[2], r)
            parts = []
            for k in range(9):
                part = poro * rows(accum.at[k], r)
                near[k, pl.ds(r, SUB), :] = part
                parts.append(part)
            stored = ((parts[0] + parts[1]) + (parts[2] + parts[3])) + ((parts[4] + parts[5]) + (parts[6] + parts[7])) + parts[8]
            near[9, pl.ds(r, SUB), :] = well
            wide[0, pl.ds(r, SUB), :] = rows(right.at[0], r) + rows(right.at[1], r) + rows(right.at[2], r)
            wide[1, pl.ds(r, SUB), :] = perm
            wide[2, pl.ds(r, SUB), :] = summed
            wide[3, pl.ds(r, SUB), :] = stored + well * summed
        a_fields = [(wide.at[0], W), (wide.at[1], W), (wide.at[2], W), (wide.at[3], W - 1)]
        b_fields = [(mobility.at[p], 2) for p in range(3)]
        b_fields += [(near.at[k], 1) for k in range(9)]
        b_fields += [(right.at[p], 1) for p in range(3)] + [(near.at[9], 1)]
        for fields, up, down in ((a_fields, a_up, a_down), (b_fields, b_up, b_down)):
            start = 0
            for ref, depth in fields:
                count = depth * ny
                up[pl.ds(start, count), :] = rows(ref, (nx - depth) * ny, count)
                down[pl.ds(start, count), :] = rows(ref, 0, count)
                start += count

    return kernel


A_PLANES = (W, W, W, W - 1)
B_PLANES = (2, 2, 2) + (1,) * 13


def side_rows(grid):
    out = []
    for field in range(4):
        reach = W if field < 3 else W - 1
        for distance in range(1, reach):
            out.append((field, distance, reach - distance))
    return out


def received(grid, planes, field, distance, side):
    start = sum(planes[:field])
    index = planes[field] - distance if side < 0 else distance - 1
    return (start + index) * grid.ny


def corner_rows(grid):
    out = []
    for side in (-1, 1):
        for field, distance, depth in side_rows(grid):
            for k in range(depth):
                out.append((0, field, side, distance, k, depth))
        for p in range(3):
            out.append((1, p, side, 1, 0, 1))
    return out


def edge_rows():
    out = []
    for field in range(4):
        reach = W if field < 3 else W - 1
        out += [(0, field, k, reach) for k in range(reach)]
    for p in range(3):
        out += [(1, p, k, 2) for k in range(2)]
    out += [(1, 3 + f, 0, 1) for f in range(13)]
    return out


def y_count(grid):
    count = len(edge_rows()) * grid.nx + len(corner_rows(grid))
    return -(-count // SUB) * SUB


def pack(grid):
    nx, ny = grid.nx, grid.ny

    def kernel(wide, near, mobility, right, a_before, a_after, b_before, b_after, up, down):
        def local(group, field):
            if group == 0:
                return wide.at[field]
            if field < 3:
                return mobility.at[field]
            field -= 3
            if field < 9:
                return near.at[field]
            return right.at[field - 9] if field < 12 else near.at[9]

        start = 0
        for group, field, k, depth in edge_rows():
            ref = local(group, field)
            up[pl.ds(start, nx), :] = ref[pl.ds(ny - depth + k, nx, stride=ny), :]
            down[pl.ds(start, nx), :] = ref[pl.ds(k, nx, stride=ny), :]
            start += nx
        for group, field, side, distance, k, depth in corner_rows(grid):
            planes = B_PLANES if group else A_PLANES
            source = ((a_before, a_after), (b_before, b_after))[group][side > 0]
            base = received(grid, planes, field, distance, side)
            up[pl.ds(start, 1), :] = rows(source, base + ny - depth + k, 1)
            down[pl.ds(start, 1), :] = rows(source, base + k, 1)
            start += 1
        left = y_count(grid) - start
        if left:
            up[pl.ds(start, left), :] = jnp.zeros((left, LANES), jnp.float32)
            down[pl.ds(start, left), :] = jnp.zeros((left, LANES), jnp.float32)

    return kernel


def spread(grid, wanted, target, local, x_before, x_after, y_before, y_after):
    nx, ny = grid.nx, grid.ny
    planes = B_PLANES if wanted else A_PLANES
    for field, depth in enumerate(planes):
        ref = target(field)
        source = local(field)
        for x in range(nx):
            ref[pl.ds(grid.at(x, 0), ny), :] = rows(source, x * ny, ny)
        for distance in range(1, depth + 1):
            ref[pl.ds(grid.at(-distance, 0), ny), :] = rows(x_before, received(grid, planes, field, distance, -1), ny)
            ref[pl.ds(grid.at(nx - 1 + distance, 0), ny), :] = rows(x_after, received(grid, planes, field, distance, 1), ny)
    start = 0
    for group, field, k, depth in edge_rows():
        if group == wanted:
            ref = target(field)
            ref[pl.ds(grid.at(0, k - depth), nx, stride=grid.pitch), :] = rows(y_before, start, nx)
            ref[pl.ds(grid.at(0, ny + k), nx, stride=grid.pitch), :] = rows(y_after, start, nx)
        start += nx
    for group, field, side, distance, k, depth in corner_rows(grid):
        if group == wanted:
            ref = target(field)
            x = -distance if side < 0 else nx - 1 + distance
            ref[pl.ds(grid.at(x, k - depth), 1), :] = rows(y_before, start, 1)
            ref[pl.ds(grid.at(x, ny + k), 1), :] = rows(y_after, start, 1)
        start += 1


def clear(ref, grid):
    for r in range(0, grid.total, SUB):
        ref[pl.ds(r, SUB), :] = jnp.zeros((SUB, LANES), jnp.float32)


def krylov(grid, devices):
    pitch = grid.pitch

    def kernel(wide, a_before, a_after, y_before, y_after, partial, v0, v1, v2, perm, summed, storage, cross_x, cross_y, cross_z):
        fields = (v0, perm, summed, storage)
        for ref in fields + (v1, v2, cross_x, cross_y, cross_z):
            clear(ref, grid)
        spread(grid, 0, lambda f: fields[f], lambda f: wide.at[f], a_before, a_after, y_before, y_after)
        inside = open_face()
        for r in grid.chunks(W):
            k, s = rows(perm, r), rows(summed, r)
            for ref, shift, scale in ((cross_x, pitch, FACE[0]), (cross_y, 1, FACE[1])):
                ref[pl.ds(r, SUB), :] = scale * harmonic(k, rows(perm, r + shift)) * (s + rows(summed, r + shift))
            cross_z[pl.ds(r, SUB), :] = (FACE[2] * inside) * harmonic(k, ahead(k)) * (s + ahead(s))

        def operate(v, r):
            here = rows(v, r)
            rise = rows(cross_z, r) * (here - ahead(here))
            out = rows(storage, r) * here + (rise - behind(rise))
            for ref, shift in ((cross_x, pitch), (cross_y, 1)):
                out = out + rows(ref, r) * (here - rows(v, r + shift))
                out = out + rows(ref, r - shift) * (here - rows(v, r - shift))
            return out

        for depth, source, target in ((W - 1, v0, v1), (W - 2, v1, v2)):
            for r in grid.chunks(depth):
                target[pl.ds(r, SUB), :] = operate(source, r)
        zero = jnp.zeros((SUB, LANES), jnp.float32)
        sums = [(zero, zero)] * MOMENTS
        for _, r in grid.core():
            basis = [rows(v0, r), rows(v1, r), rows(v2, r), operate(v2, r)]
            parts = [split(b) for b in basis]
            for k in range(MOMENTS):
                i, j = k // 2, k - k // 2
                product, error = two_prod(basis[i], basis[j], parts[i], parts[j])
                total, lost = two_sum(sums[k][0], product)
                sums[k] = (total, sums[k][1] + (lost + error))
        for shift in (4, 2, 1):
            sums = [pair_add(s, tuple(pltpu.roll(part, shift, 0) for part in s)) for s in sums]
        sub = lax.broadcasted_iota(jnp.int32, (SUB, LANES), 0)
        lane = lax.broadcasted_iota(jnp.int32, (SUB, LANES), 1)
        high, low = zero, zero
        for k, s in enumerate(sums):
            high = jnp.where(sub == k, s[0], high)
            low = jnp.where(sub == k, s[1], low)
        pair = (high, low)
        shift = LANES // 2
        while shift:
            pair = pair_add(pair, tuple(pltpu.roll(part, shift, 1) for part in pair))
            shift //= 2
        picked = jnp.where(lane == sub, pair[0], 0.0) + jnp.where(lane == sub + LOW, pair[1], 0.0)
        for shift in (4, 2, 1):
            picked = picked + pltpu.roll(picked, shift, 0)
        row = picked[0:1]

        def put(i, carry):
            partial[i] = row
            return carry

        lax.fori_loop(0, devices, put, 0, unroll=devices <= 64)

    return kernel


def precompute(grid):
    pitch = grid.pitch

    def kernel(near, mobility, right, b_before, b_after, y_before, y_after, perm, cross, inverse, sums, block, source, well, mobile):
        def target(field):
            if field < 3:
                return mobile.at[field]
            field -= 3
            if field < 9:
                return block.at[field]
            return source.at[field - 9] if field < 12 else well

        def local(field):
            if field < 3:
                return mobility.at[field]
            field -= 3
            if field < 9:
                return near.at[field]
            return right.at[field - 9] if field < 12 else near.at[9]

        spread(grid, 1, target, local, b_before, b_after, y_before, y_after)
        inside = open_face()
        for r in grid.chunks(2):
            k = rows(perm, r)
            along_x = FACE[0] * harmonic(k, rows(perm, r + pitch))
            along_y = FACE[1] * harmonic(k, rows(perm, r + 1))
            along_z = (FACE[2] * inside) * harmonic(k, ahead(k))
            for p in range(3):
                m = rows(mobile.at[p], r)
                cross[p, pl.ds(r, SUB), :] = along_x * (m + rows(mobile.at[p], r + pitch))
                cross[3 + p, pl.ds(r, SUB), :] = along_y * (m + rows(mobile.at[p], r + 1))
                cross[6 + p, pl.ds(r, SUB), :] = along_z * (m + ahead(m))
        for r in grid.chunks(1):
            drain = rows(well, r)
            blocks = [[rows(block.at[3 * p + q], r) for q in range(3)] for p in range(3)]
            for p in range(3):
                up = rows(cross.at[6 + p], r)
                flow = rows(cross.at[p], r) + rows(cross.at[p], r - pitch)
                flow = flow + rows(cross.at[3 + p], r) + rows(cross.at[3 + p], r - 1)
                flow = flow + up + behind(up)
                phase = drain * rows(mobile.at[p], r)
                sums[p, pl.ds(r, SUB), :] = (blocks[p][0] + blocks[p][1]) + (blocks[p][2] + phase)
                block[3 * p + p, pl.ds(r, SUB), :] = blocks[p][p] + phase
                blocks[p][p] = blocks[p][p] + (flow + phase)

            def cofactor(i, j):
                a, b, c, d = (i + 1) % 3, (i + 2) % 3, (j + 1) % 3, (j + 2) % 3
                return blocks[a][c] * blocks[b][d] - blocks[a][d] * blocks[b][c]

            adjugate = [[cofactor(j, i) for j in range(3)] for i in range(3)]
            determinant = blocks[0][0] * adjugate[0][0] + blocks[0][1] * adjugate[1][0] + blocks[0][2] * adjugate[2][0]
            scale = 1.0 / jnp.where(determinant == 0.0, 1.0, determinant)
            for i in range(3):
                for j in range(3):
                    inverse[3 * i + j, pl.ds(r, SUB), :] = adjugate[i][j] * scale

    return kernel


def finish(grid, devices):
    pitch = grid.pitch

    def kernel(gathered, v0, v1, v2, cross, inverse, sums, block, source, pressure_out, correction, pressure, update):
        if devices <= 64:
            terms = [(gathered[i], jnp.zeros((1, LANES), jnp.float32)) for i in range(devices)]
            total = pair_tree(terms)
        else:
            zero = jnp.zeros((1, LANES), jnp.float32)
            total = lax.fori_loop(0, devices, lambda i, t: pair_add(t, (gathered[i], zero)), (zero, zero))
        moments = []
        for k in range(MOMENTS):
            high, low = (jnp.broadcast_to(t[:, k : k + 1], (SUB, LANES)) for t in total)
            rest, _ = (jnp.broadcast_to(t[:, LOW + k : LOW + k + 1], (SUB, LANES)) for t in total)
            moments.append(pair_add((high, low), (rest, jnp.zeros_like(rest))))
        weights = combination(moments)
        for r in grid.chunks(2):
            pressure[pl.ds(r, SUB), :] = (
                weights[0] * rows(v0, r) + weights[1] * rows(v1, r) + weights[2] * rows(v2, r)
            )
        for start, r in grid.core():
            pressure_out[pl.ds(start, SUB), :] = rows(pressure, r)

        def solve(r, defects):
            return [
                rows(inverse.at[3 * p], r) * defects[0]
                + rows(inverse.at[3 * p + 1], r) * defects[1]
                + rows(inverse.at[3 * p + 2], r) * defects[2]
                for p in range(3)
            ]

        for r in grid.chunks(1):
            here = rows(pressure, r)
            east, west = here - rows(pressure, r + pitch), here - rows(pressure, r - pitch)
            north, south = here - rows(pressure, r + 1), here - rows(pressure, r - 1)
            rise = here - ahead(here)
            defects = []
            for p in range(3):
                lift = rows(cross.at[6 + p], r) * rise
                image = rows(sums.at[p], r) * here + (lift - behind(lift))
                image = image + (rows(cross.at[p], r) * east + rows(cross.at[p], r - pitch) * west)
                image = image + (rows(cross.at[3 + p], r) * north + rows(cross.at[3 + p], r - 1) * south)
                defects.append(rows(source.at[p], r) - image)
            for p, change in enumerate(solve(r, defects)):
                update[p, pl.ds(r, SUB), :] = here + change
        for start, r in grid.core():
            here = [rows(update.at[p], r) for p in range(3)]
            defects = []
            for p in range(3):
                field = update.at[p]
                lift = rows(cross.at[6 + p], r) * (here[p] - ahead(here[p]))
                image = lift - behind(lift)
                for q in range(3):
                    image = image + rows(block.at[3 * p + q], r) * here[q]
                for base, shift in ((p, pitch), (3 + p, 1)):
                    image = image + rows(cross.at[base], r) * (here[p] - rows(field, r + shift))
                    image = image + rows(cross.at[base], r - shift) * (here[p] - rows(field, r - shift))
                defects.append(rows(source.at[p], r) - image)
            for p, change in enumerate(solve(r, defects)):
                correction[p, pl.ds(start, SUB), :] = here[p] + change

    return kernel


def shift_both(up_payload, down_payload, axis):
    devices = lax.axis_size(axis)
    up = [(i, (i + 1) % devices) for i in range(devices - 1)]
    down = [(j, i) for i, j in up]
    return lax.ppermute(up_payload, axis, up), lax.ppermute(down_payload, axis, down)


def shards(rock_class, well_mask, perm_table, poro_table, accum, mobility, right_side):
    nx, ny, nz = rock_class.shape
    grid = Grid(nx, ny)
    devices = lax.axis_size("gx") * lax.axis_size("gy")
    block = (grid.rows, nz)
    extended = (grid.total, nz)
    rock, mask = rock_class.reshape(block), well_mask.reshape(block)
    accum = accum.reshape((9,) + block)
    mobility = mobility.reshape((3,) + block)
    right = right_side.reshape((3,) + block)
    a_rows, b_rows = (sum(A_PLANES) * ny, nz), (sum(B_PLANES) * ny, nz)
    wide, near, a_up, a_down, b_up, b_down = call(
        prepare(grid, perm_table.shape[0]),
        "prepare",
        [(4,) + block, (10,) + block, a_rows, a_rows, b_rows, b_rows],
        perm_table,
        poro_table,
        rock,
        mask,
        accum,
        mobility,
        right,
        specs=[SMEM, SMEM] + [VMEM] * 5,
    )
    a_before, a_after = shift_both(a_up, a_down, "gx")
    b_before, b_after = shift_both(b_up, b_down, "gx")
    y_rows = (y_count(grid), nz)
    y_up, y_down = call(pack(grid), "pack", [y_rows, y_rows], wide, near, mobility, right, a_before, a_after, b_before, b_after)
    y_before, y_after = shift_both(y_up, y_down, "gy")
    scratch = pltpu.VMEM(extended, jnp.float32)
    partial, v0, v1, v2, perm = call(
        krylov(grid, devices),
        "krylov",
        [(devices, 1, nz)] + [extended] * 4,
        wide,
        a_before,
        a_after,
        y_before,
        y_after,
        scratch=[scratch] * 5,
    )
    gathered = lax.all_to_all(partial, ("gx", "gy"), 0, 0)
    nine, three = (9,) + extended, (3,) + extended
    cross, inverse, sums, blocks, source = call(
        precompute(grid),
        "precompute",
        [nine, nine, three, nine, three],
        near,
        mobility,
        right,
        b_before,
        b_after,
        y_before,
        y_after,
        perm,
        scratch=[scratch, pltpu.VMEM(three, jnp.float32)],
    )
    pressure, correction = call(
        finish(grid, devices),
        "finish",
        [block, (3,) + block],
        gathered,
        v0,
        v1,
        v2,
        cross,
        inverse,
        sums,
        blocks,
        source,
        scratch=[scratch, pltpu.VMEM(three, jnp.float32)],
    )
    return pressure.reshape(nx, ny, nz), correction.reshape(3, nx, ny, nz)


def solution(mesh):
    return jax.shard_map(
        shards,
        mesh=mesh,
        in_specs=(
            P("gx", "gy", None),
            P("gx", "gy", None),
            P(),
            P(),
            P(None, None, "gx", "gy", None),
            P(None, "gx", "gy", None),
            P(None, "gx", "gy", None),
        ),
        out_specs=(P("gx", "gy", None), P(None, "gx", "gy", None)),
        check_vma=False,
    )
```

time: 230 us -> 55.9 us (0.24)
  the two profiles are of different devices: /device:TPU:12 before, /device:TPU:0 now
where the time goes in v2:
time: 55.9 us; the launch traced here: 55.5 us
  starting transfers between devices  22.9 us (41%)
  Pallas kernels  18 us (32%)
  waiting for transfers between devices  11.9 us (21%)
  local copies, waits for them, and re-layouts  2.02 us (4%)
  between operations  0.73 us (1%)
    pallas_call x5, Pallas kernels, call(): pl.pallas_call(kernel, name=name, out_shape=out, in_specs=specs or [VMEM]...  18 us
    ppermute x3, starting transfers between devices, shift_both(): lax.ppermute(up_payload, axis, up)  10.8 us
    all_to_all x1, starting transfers between devices, shards(): gathered = lax.all_to_all(partial, ('gx', 'gy'), 0, 0)  8.23 us
    ppermute x3, waiting for transfers between devices, shift_both(): lax.ppermute(down_payload, axis, down)  8.14 us
    ppermute x3, starting transfers between devices, shift_both(): lax.ppermute(down_payload, axis, down)  3.88 us
    all_to_all x1, waiting for transfers between devices, shards(): gathered = lax.all_to_all(partial, ('gx', 'gy'), 0, 0)  2.27 us
    unnamed x14, local copies, waits for them, and re-layouts  2.02 us
    ppermute x3, waiting for transfers between devices, shift_both(): lax.ppermute(up_payload, axis, up)  1.44 us
  transfers between devices with their start and end apart: 7, of which 4 were waited for; matrix products, arithmetic and copies ran while one was open for 0% of the time, Pallas kernels for 9%

profile of v2, /device:TPU:0, one launch (start us, length us, event | category | flops | bytes accessed | tf_op | source)
XLA Modules:
  0.0 55.5 jit_solution(2505778900407628938)
XLA Ops:
  0.6 2.5 %prepare.1 = (f32[4,128,128]{2,1,0:T(8,128)}, f32[10,128,128]{2,1,0:T(8,128)}, f32[240,128]{1,0:T(8,128)}, f32[240,128]{1,0:T(8,128)}, f32[304,128]{1,0:T(8,128)}, /*index=5*/f32[304,128]{1,0:T(8,128)}) custom-call(f32[16]{0:T(128)} %perm_table.1, f32[16]{0:T(128)} %poro_table.1, s32[128,128]{1,0:T(8,128)} %bitcast.14, s32[128,128]{1,0:T(8,128)} %bitcast.15, ...), custom_call_target="tpu_custom_call" | custom-call | tf_op jit(solution)/shard_map/prepare/pallas_call | solution.py:25
  3.2 5.0 %collective-permute-start.2 = (f32[304,128]{1,0:T(8,128)}, f32[304,128]{1,0:T(8,128)S(1)}, u32[]{:S(2)}, u32[]{:S(2)}) collective-permute-start(f32[304,128]{1,0:T(8,128)} %get-tuple-element.26), channel_id=1, source_target_pairs={{0,8},{8,16},{16,24},{1,9},{9,17},{17,25},{2,10},{10,18},{18,26},{... | collective-permute-start | bytes 466952 | tf_op jit(solution)/shard_map/ppermute | solution.py:507
  8.1 1.3 %collective-permute-start.3 = (f32[304,128]{1,0:T(8,128)}, f32[304,128]{1,0:T(8,128)S(1)}, u32[]{:S(2)}, u32[]{:S(2)}) collective-permute-start(f32[304,128]{1,0:T(8,128)} %get-tuple-element.27), channel_id=1, source_target_pairs={{8,0},{16,8},{24,16},{9,1},{17,9},{25,17},{10,2},{18,10},{26,18},{... | collective-permute-start | bytes 466952 | tf_op jit(solution)/shard_map/ppermute | solution.py:507
  9.4 4.6 %collective-permute-start = (f32[240,128]{1,0:T(8,128)}, f32[240,128]{1,0:T(8,128)S(1)}, u32[]{:S(2)}, u32[]{:S(2)}) collective-permute-start(f32[240,128]{1,0:T(8,128)} %get-tuple-element.23), channel_id=1, source_target_pairs={{0,8},{8,16},{16,24},{1,9},{9,17},{17,25},{2,10},{10,18},{18,26},{... | collective-permute-start | bytes 368648 | tf_op jit(solution)/shard_map/ppermute | solution.py:507
  14.0 1.3 %collective-permute-start.1 = (f32[240,128]{1,0:T(8,128)}, f32[240,128]{1,0:T(8,128)S(1)}, u32[]{:S(2)}, u32[]{:S(2)}) collective-permute-start(f32[240,128]{1,0:T(8,128)} %get-tuple-element.24), channel_id=1, source_target_pairs={{8,0},{16,8},{24,16},{9,1},{17,9},{25,17},{10,2},{18,10},{26,18},{... | collective-permute-start | bytes 368648 | tf_op jit(solution)/shard_map/ppermute | solution.py:507
  15.3 1.4 %collective-permute-done.a_before = f32[240,128]{1,0:T(8,128)S(1)} collective-permute-done((f32[240,128]{1,0:T(8,128)}, f32[240,128]{1,0:T(8,128)S(1)}, u32[]{:S(2)}, u32[]{:S(2)}) %collective-permute-start) | collective-permute-done | bytes 122912 | tf_op jit(solution)/shard_map/ppermute | solution.py:507
  16.7 0.0 copy-start.4
  16.7 4.2 %collective-permute-done.1.a_after = f32[240,128]{1,0:T(8,128)S(1)} collective-permute-done((f32[240,128]{1,0:T(8,128)}, f32[240,128]{1,0:T(8,128)S(1)}, u32[]{:S(2)}, u32[]{:S(2)}) %collective-permute-start.1) | collective-permute-done | bytes 122912 | tf_op jit(solution)/shard_map/ppermute | solution.py:507
  21.0 0.0 copy-start.5
  21.0 0.0 collective-permute-done.2.b_before
  21.0 0.0 copy-start.2
  21.0 0.0 collective-permute-done.3.b_after
  21.0 0.0 copy-start.3
  21.0 0.0 copy-done.4
  21.0 0.6 %copy-done.5 = f32[240,128]{1,0:T(8,128)} copy-done((f32[240,128]{1,0:T(8,128)}, f32[240,128]{1,0:T(8,128)S(1)}, u32[]{:S(2)}) %copy-start.5) | copy-done | bytes 122904
  21.6 0.1 copy-done.2
  21.7 0.1 copy-done.3
  21.7 2.3 %pack.1 = (f32[320,128]{1,0:T(8,128)}, f32[320,128]{1,0:T(8,128)}) custom-call(f32[4,128,128]{2,1,0:T(8,128)} %get-tuple-element.22.wide, f32[10,128,128]{2,1,0:T(8,128)} %get-tuple-element.25.near, f32[3,128,128]{2,1,0:T(8,128)} %bitcast.8, f32[3,128,128]{2,1,0:T(8,128)} %bitcast.11, f32[240,128]{1,0:T(8,128)} %copy-done.4, f32[240,128]{1,0:T(8,128)} %copy-done.5, ...), custom_call_target="tpu_custom_call" | custom-call | tf_op jit(solution)/shard_map/pack/pallas_call | solution.py:25
  24.0 1.3 %collective-permute-start.4 = (f32[320,128]{1,0:T(8,128)}, f32[320,128]{1,0:T(8,128)S(1)}, u32[]{:S(2)}, u32[]{:S(2)}) collective-permute-start(f32[320,128]{1,0:T(8,128)} %get-tuple-element.28), channel_id=1, source_target_pairs={{0,1},{1,2},{2,3},{3,4},{4,5},{5,6},{6,7},{8,9},{9,10},{10,11},{11... | collective-permute-start | bytes 491528 | tf_op jit(solution)/shard_map/ppermute | solution.py:507
  25.3 1.3 %collective-permute-start.5 = (f32[320,128]{1,0:T(8,128)}, f32[320,128]{1,0:T(8,128)S(1)}, u32[]{:S(2)}, u32[]{:S(2)}) collective-permute-start(f32[320,128]{1,0:T(8,128)} %get-tuple-element.29), channel_id=1, source_target_pairs={{1,0},{2,1},{3,2},{4,3},{5,4},{6,5},{7,6},{9,8},{10,9},{11,10},{12... | collective-permute-start | bytes 491528 | tf_op jit(solution)/shard_map/ppermute | solution.py:507
  26.6 0.0 collective-permute-done.4.y_before
  26.6 0.0 copy-start
  26.6 3.9 %collective-permute-done.5.y_after = f32[320,128]{1,0:T(8,128)S(1)} collective-permute-done((f32[320,128]{1,0:T(8,128)}, f32[320,128]{1,0:T(8,128)S(1)}, u32[]{:S(2)}, u32[]{:S(2)}) %collective-permute-start.5) | collective-permute-done | bytes 163872 | tf_op jit(solution)/shard_map/ppermute | solution.py:507
  30.5 0.0 copy-done
  30.5 0.0 copy-start.1
  30.5 0.7 %copy-done.1 = f32[320,128]{1,0:T(8,128)} copy-done((f32[320,128]{1,0:T(8,128)}, f32[320,128]{1,0:T(8,128)S(1)}, u32[]{:S(2)}) %copy-start.1) | copy-done | bytes 163864
  31.2 3.4 %krylov.1 = (f32[32,1,128]{2,1,0:T(1,128)}, f32[440,128]{1,0:T(8,128)}, f32[440,128]{1,0:T(8,128)}, f32[440,128]{1,0:T(8,128)}, f32[440,128]{1,0:T(8,128)}) custom-call(f32[4,128,128]{2,1,0:T(8,128)} %get-tuple-element.22.wide, f32[240,128]{1,0:T(8,128)} %copy-done.4, f32[240,128]{1,0:T(8,128)} %copy-done.5, f32[320,128]{1,0:T(8,128)} %copy-done, ...), custom_call_target="tpu_custom_call" | custom-call | tf_op jit(solution)/shard_map/krylov/pallas_call | solution.py:25
  34.5 8.2 %all-to-all-start = ((f32[32,1,128]{2,1,0:T(1,128)}), f32[32,1,128]{2,1,0:T(1,128)S(1)}, u32[]{:S(2)}, u32[]{:S(2)}) async-start(f32[32,1,128]{2,1,0:T(1,128)} %get-tuple-element.30), calls=%async_computation | async-start | bytes 32768 | tf_op jit(solution)/shard_map/all_to_all | solution.py:551
  42.8 4.8 %precompute.1 = (f32[9,440,128]{2,1,0:T(8,128)}, f32[9,440,128]{2,1,0:T(8,128)}, f32[3,440,128]{2,1,0:T(8,128)}, f32[9,440,128]{2,1,0:T(8,128)}, f32[3,440,128]{2,1,0:T(8,128)}) custom-call(f32[10,128,128]{2,1,0:T(8,128)} %get-tuple-element.25.near, f32[3,128,128]{2,1,0:T(8,128)} %bitcast.9, f32[3,128,128]{2,1,0:T(8,128)} %bitcast.12, f32[304,128]{1,0:T(8,128)} %copy-done.2, ...), custom_call_target="tpu_custom_call" | custom-call | tf_op jit(solution)/shard_map/precompute/pallas_call | solution.py:25
  47.6 2.3 %all-to-all-done.gathered = f32[32,1,128]{2,1,0:T(1,128)S(1)} async-done(((f32[32,1,128]{2,1,0:T(1,128)}), f32[32,1,128]{2,1,0:T(1,128)S(1)}, u32[]{:S(2)}, u32[]{:S(2)}) %all-to-all-start) | async-done | bytes 16416 | tf_op jit(solution)/shard_map/all_to_all | solution.py:551
  49.9 0.6 %copy-done.6 = f32[32,1,128]{2,1,0:T(1,128)} copy-done((f32[32,1,128]{2,1,0:T(1,128)}, f32[32,1,128]{2,1,0:T(1,128)S(1)}, u32[]{:S(2)}) %copy-start.6) | copy-done | bytes 16408
  50.5 5.0 %finish.1 = (f32[128,128]{1,0:T(8,128)}, f32[3,128,128]{2,1,0:T(8,128)}) custom-call(f32[32,1,128]{2,1,0:T(1,128)} %copy-done.6, f32[440,128]{1,0:T(8,128)} %get-tuple-element.31.v0, f32[440,128]{1,0:T(8,128)} %get-tuple-element.32.v1, f32[440,128]{1,0:T(8,128)} %get-tuple-element.33.v2, f32[9,440,128]{2,1,0:T(8,128)} %get-tuple-element.35.cross, ...), custom_call_target="tpu_custom_call" | custom-call | tf_op jit(solution)/shard_map/finish/pallas_call | solution.py:25
  (1 shorter events, 0.0 us)
Async XLA Ops:
  3.2 17.8 %collective-permute-start.2 = (f32[304,128]{1,0:T(8,128)}, f32[304,128]{1,0:T(8,128)S(1)}, u32[]{:S(2)}, u32[]{:S(2)}) collective-permute-start(f32[304,128]{1,0:T(8,128)} %get-tuple-element.26), channel_id=1, source_target_pairs={{0,8},{8,16},{16,24},{1,9},{9,17},{17,25},{2,10},{10,18},{18,26},{... | collective-permute-start | bytes 466952 | tf_op jit(solution)/shard_map/ppermute | solution.py:507
  8.1 12.9 %collective-permute-start.3 = (f32[304,128]{1,0:T(8,128)}, f32[304,128]{1,0:T(8,128)S(1)}, u32[]{:S(2)}, u32[]{:S(2)}) collective-permute-start(f32[304,128]{1,0:T(8,128)} %get-tuple-element.27), channel_id=1, source_target_pairs={{8,0},{16,8},{24,16},{9,1},{17,9},{25,17},{10,2},{18,10},{26,18},{... | collective-permute-start | bytes 466952 | tf_op jit(solution)/shard_map/ppermute | solution.py:507
  9.4 7.3 %collective-permute-start = (f32[240,128]{1,0:T(8,128)}, f32[240,128]{1,0:T(8,128)S(1)}, u32[]{:S(2)}, u32[]{:S(2)}) collective-permute-start(f32[240,128]{1,0:T(8,128)} %get-tuple-element.23), channel_id=1, source_target_pairs={{0,8},{8,16},{16,24},{1,9},{9,17},{17,25},{2,10},{10,18},{18,26},{... | collective-permute-start | bytes 368648 | tf_op jit(solution)/shard_map/ppermute | solution.py:507
  14.0 7.0 %collective-permute-start.1 = (f32[240,128]{1,0:T(8,128)}, f32[240,128]{1,0:T(8,128)S(1)}, u32[]{:S(2)}, u32[]{:S(2)}) collective-permute-start(f32[240,128]{1,0:T(8,128)} %get-tuple-element.24), channel_id=1, source_target_pairs={{8,0},{16,8},{24,16},{9,1},{17,9},{25,17},{10,2},{18,10},{26,18},{... | collective-permute-start | bytes 368648 | tf_op jit(solution)/shard_map/ppermute | solution.py:507
  16.7 4.3 %copy-start.4 = (f32[240,128]{1,0:T(8,128)}, f32[240,128]{1,0:T(8,128)S(1)}, u32[]{:S(2)}) copy-start(f32[240,128]{1,0:T(8,128)S(1)} %collective-permute-done.a_before) | copy-start | bytes 368644
  21.0 0.6 %copy-start.5 = (f32[240,128]{1,0:T(8,128)}, f32[240,128]{1,0:T(8,128)S(1)}, u32[]{:S(2)}) copy-start(f32[240,128]{1,0:T(8,128)S(1)} %collective-permute-done.1.a_after) | copy-start | bytes 368644
  21.0 0.7 %copy-start.2 = (f32[304,128]{1,0:T(8,128)}, f32[304,128]{1,0:T(8,128)S(1)}, u32[]{:S(2)}) copy-start(f32[304,128]{1,0:T(8,128)S(1)} %collective-permute-done.2.b_before) | copy-start | bytes 466948
  21.0 0.8 %copy-start.3 = (f32[304,128]{1,0:T(8,128)}, f32[304,128]{1,0:T(8,128)S(1)}, u32[]{:S(2)}) copy-start(f32[304,128]{1,0:T(8,128)S(1)} %collective-permute-done.3.b_after) | copy-start | bytes 466948
  24.0 2.6 %collective-permute-start.4 = (f32[320,128]{1,0:T(8,128)}, f32[320,128]{1,0:T(8,128)S(1)}, u32[]{:S(2)}, u32[]{:S(2)}) collective-permute-start(f32[320,128]{1,0:T(8,128)} %get-tuple-element.28), channel_id=1, source_target_pairs={{0,1},{1,2},{2,3},{3,4},{4,5},{5,6},{6,7},{8,9},{9,10},{10,11},{11... | collective-permute-start | bytes 491528 | tf_op jit(solution)/shard_map/ppermute | solution.py:507
  25.3 5.2 %collective-permute-start.5 = (f32[320,128]{1,0:T(8,128)}, f32[320,128]{1,0:T(8,128)S(1)}, u32[]{:S(2)}, u32[]{:S(2)}) collective-permute-start(f32[320,128]{1,0:T(8,128)} %get-tuple-element.29), channel_id=1, source_target_pairs={{1,0},{2,1},{3,2},{4,3},{5,4},{6,5},{7,6},{9,8},{10,9},{11,10},{12... | collective-permute-start | bytes 491528 | tf_op jit(solution)/shard_map/ppermute | solution.py:507
  26.6 3.9 %copy-start = (f32[320,128]{1,0:T(8,128)}, f32[320,128]{1,0:T(8,128)S(1)}, u32[]{:S(2)}) copy-start(f32[320,128]{1,0:T(8,128)S(1)} %collective-permute-done.4.y_before) | copy-start | bytes 491524
  30.5 0.7 %copy-start.1 = (f32[320,128]{1,0:T(8,128)}, f32[320,128]{1,0:T(8,128)S(1)}, u32[]{:S(2)}) copy-start(f32[320,128]{1,0:T(8,128)S(1)} %collective-permute-done.5.y_after) | copy-start | bytes 491524
  34.5 15.3 %all-to-all-start = ((f32[32,1,128]{2,1,0:T(1,128)}), f32[32,1,128]{2,1,0:T(1,128)S(1)}, u32[]{:S(2)}, u32[]{:S(2)}) async-start(f32[32,1,128]{2,1,0:T(1,128)} %get-tuple-element.30), calls=%async_computation | async-start | bytes 32768 | tf_op jit(solution)/shard_map/all_to_all | solution.py:551
  49.9 0.6 %copy-start.6 = (f32[32,1,128]{2,1,0:T(1,128)}, f32[32,1,128]{2,1,0:T(1,128)S(1)}, u32[]{:S(2)}) copy-start(f32[32,1,128]{2,1,0:T(1,128)S(1)} %all-to-all-done.gathered) | copy-start | bytes 49156

commit v3 on v2

--- a/solution.py
+++ b/solution.py
@@ -13,6 +13,7 @@
 MOMENTS = 2 * ITERS
 LOW = 8
 STOP = 1e-12
+SCOPED = 24 * 1024 * 1024
 LANES = 128
 SUB = 8
 
@@ -20,8 +21,9 @@
 SMEM = pl.BlockSpec(memory_space=pltpu.SMEM)
 
 
-def call(kernel, name, shapes, *operands, specs=None, scratch=()):
-    out = [jax.ShapeDtypeStruct(shape, jnp.float32) for shape in shapes]
+def call(kernel, name, shapes, *operands, specs=None, scratch=(), resident=True):
+    kind = pltpu.VMEM if resident else jax.ShapeDtypeStruct
+    out = [kind(shape, jnp.float32) for shape in shapes]
     return pl.pallas_call(
         kernel,
         name=name,
@@ -29,6 +31,7 @@
         in_specs=specs or [VMEM] * len(operands),
         out_specs=[VMEM] * len(out),
         scratch_shapes=list(scratch),
+        compiler_params=pltpu.CompilerParams(vmem_limit_bytes=SCOPED),
     )(*operands)
 
 
@@ -160,10 +163,42 @@
     return result
 
 
+A_PLANES = (W, W, W, W - 1)
+B_PLANES = (2, 2, 2) + (1,) * 13
+
+
+def send_planes(grid, fields, up, down):
+    start = 0
+    for ref, depth in fields:
+        count = depth * grid.ny
+        up[pl.ds(start, count), :] = rows(ref, (grid.nx - depth) * grid.ny, count)
+        down[pl.ds(start, count), :] = rows(ref, 0, count)
+        start += count
+    return start
+
+
 def prepare(grid, classes):
     nx, ny = grid.nx, grid.ny
 
-    def kernel(perm_table, poro_table, rock, mask, accum, mobility, right, wide, near, a_up, a_down, b_up, b_down):
+    def kernel(
+        perm_table, poro_table, rock_in, mask_in, accum_in, mobility_in, right_in,
+        wide, near, mobility, right, a_up, a_down, rock, mask, arrived,
+    ):
+        copies = [
+            pltpu.make_async_copy(source, target, arrived.at[i])
+            for i, (source, target) in enumerate(
+                (
+                    (rock_in, rock),
+                    (mask_in, mask),
+                    (mobility_in, mobility),
+                    (right_in, right),
+                    (accum_in, near.at[pl.ds(0, 9)]),
+                )
+            )
+        ]
+        for copy in copies:
+            copy.start()
+        copies[0].wait()
         for r in range(0, grid.rows, SUB):
             kind = rows(rock, r)
             perm = jnp.zeros((SUB, LANES), jnp.float32)
@@ -172,36 +207,34 @@
                 hit = kind == k
                 perm = jnp.where(hit, perm_table[k], perm)
                 poro = jnp.where(hit, poro_table[k], poro)
-            well = (WELL_FACTOR * perm) * rows(mask, r).astype(jnp.float32)
-            summed = rows(mobility.at[0], r) + rows(mobility.at[1], r) + rows(mobility.at[2], r)
+            wide[1, pl.ds(r, SUB), :] = perm
+            wide[3, pl.ds(r, SUB), :] = poro
+        for copy in copies[1:4]:
+            copy.wait()
+        for r in range(0, grid.rows, SUB):
+            near[9, pl.ds(r, SUB), :] = (WELL_FACTOR * rows(wide.at[1], r)) * rows(mask, r).astype(jnp.float32)
+            for out, fields in ((0, right), (2, mobility)):
+                wide[out, pl.ds(r, SUB), :] = rows(fields.at[0], r) + rows(fields.at[1], r) + rows(fields.at[2], r)
+        copies[4].wait()
+        for r in range(0, grid.rows, SUB):
+            poro = rows(wide.at[3], r)
             parts = []
             for k in range(9):
-                part = poro * rows(accum.at[k], r)
+                part = poro * rows(near.at[k], r)
                 near[k, pl.ds(r, SUB), :] = part
                 parts.append(part)
             stored = ((parts[0] + parts[1]) + (parts[2] + parts[3])) + ((parts[4] + parts[5]) + (parts[6] + parts[7])) + parts[8]
-            near[9, pl.ds(r, SUB), :] = well
-            wide[0, pl.ds(r, SUB), :] = rows(right.at[0], r) + rows(right.at[1], r) + rows(right.at[2], r)
-            wide[1, pl.ds(r, SUB), :] = perm
-            wide[2, pl.ds(r, SUB), :] = summed
-            wide[3, pl.ds(r, SUB), :] = stored + well * summed
-        a_fields = [(wide.at[0], W), (wide.at[1], W), (wide.at[2], W), (wide.at[3], W - 1)]
-        b_fields = [(mobility.at[p], 2) for p in range(3)]
-        b_fields += [(near.at[k], 1) for k in range(9)]
-        b_fields += [(right.at[p], 1) for p in range(3)] + [(near.at[9], 1)]
-        for fields, up, down in ((a_fields, a_up, a_down), (b_fields, b_up, b_down)):
-            start = 0
-            for ref, depth in fields:
-                count = depth * ny
-                up[pl.ds(start, count), :] = rows(ref, (nx - depth) * ny, count)
-                down[pl.ds(start, count), :] = rows(ref, 0, count)
-                start += count
+            wide[3, pl.ds(r, SUB), :] = stored + rows(near.at[9], r) * rows(wide.at[2], r)
+        fields = [(wide.at[f], depth) for f, depth in enumerate(A_PLANES)]
+        start = send_planes(grid, fields, a_up, a_down)
+        for p in range(3):
+            for k, y in enumerate((0, ny - 1)):
+                a_up[pl.ds(start + 2 * p + k, 1), :] = rows(mobility.at[p], (nx - 1) * ny + y, 1)
+                a_down[pl.ds(start + 2 * p + k, 1), :] = rows(mobility.at[p], y, 1)
+        for ref in (a_up, a_down):
+            ref[pl.ds(start + 6, 2), :] = jnp.zeros((2, LANES), jnp.float32)
 
     return kernel
-
-
-A_PLANES = (W, W, W, W - 1)
-B_PLANES = (2, 2, 2) + (1,) * 13
 
 
 def side_rows(grid):
@@ -249,16 +282,12 @@
 def pack(grid):
     nx, ny = grid.nx, grid.ny
 
-    def kernel(wide, near, mobility, right, a_before, a_after, b_before, b_after, up, down):
+    def kernel(wide, near, mobility, right, a_before, a_after, up, down, b_up, b_down):
+        later = [mobility.at[p] for p in range(3)] + [near.at[k] for k in range(9)]
+        later += [right.at[p] for p in range(3)] + [near.at[9]]
+
         def local(group, field):
-            if group == 0:
-                return wide.at[field]
-            if field < 3:
-                return mobility.at[field]
-            field -= 3
-            if field < 9:
-                return near.at[field]
-            return right.at[field - 9] if field < 12 else near.at[9]
+            return later[field] if group else wide.at[field]
 
         start = 0
         for group, field, k, depth in edge_rows():
@@ -267,16 +296,21 @@
             down[pl.ds(start, nx), :] = ref[pl.ds(k, nx, stride=ny), :]
             start += nx
         for group, field, side, distance, k, depth in corner_rows(grid):
-            planes = B_PLANES if group else A_PLANES
-            source = ((a_before, a_after), (b_before, b_after))[group][side > 0]
-            base = received(grid, planes, field, distance, side)
-            up[pl.ds(start, 1), :] = rows(source, base + ny - depth + k, 1)
-            down[pl.ds(start, 1), :] = rows(source, base + k, 1)
+            source = a_after if side > 0 else a_before
+            if group:
+                base = sum(A_PLANES) * ny + 2 * field
+                high, low = base + 1, base
+            else:
+                base = received(grid, A_PLANES, field, distance, side)
+                high, low = base + ny - depth + k, base + k
+            up[pl.ds(start, 1), :] = rows(source, high, 1)
+            down[pl.ds(start, 1), :] = rows(source, low, 1)
             start += 1
         left = y_count(grid) - start
         if left:
             up[pl.ds(start, left), :] = jnp.zeros((left, LANES), jnp.float32)
             down[pl.ds(start, left), :] = jnp.zeros((left, LANES), jnp.float32)
+        send_planes(grid, list(zip(later, B_PLANES)), b_up, b_down)
 
     return kernel
 
@@ -380,7 +414,7 @@
 def precompute(grid):
     pitch = grid.pitch
 
-    def kernel(near, mobility, right, b_before, b_after, y_before, y_after, perm, cross, inverse, sums, block, source, well, mobile):
+    def kernel(near, mobility, right, b_before, b_after, y_before, y_after, perm, v0, v1, v2, swept, cross, inverse, sums, block, source, well, mobile, update):
         def target(field):
             if field < 3:
                 return mobile.at[field]
@@ -433,13 +467,53 @@
                 for j in range(3):
                     inverse[3 * i + j, pl.ds(r, SUB), :] = adjugate[i][j] * scale
 
+        def solve(r, defects):
+            return [
+                rows(inverse.at[3 * p], r) * defects[0]
+                + rows(inverse.at[3 * p + 1], r) * defects[1]
+                + rows(inverse.at[3 * p + 2], r) * defects[2]
+                for p in range(3)
+            ]
+
+        for r in grid.chunks(1):
+            for i, v in enumerate((v0, v1, v2)):
+                here = rows(v, r)
+                east, west = here - rows(v, r + pitch), here - rows(v, r - pitch)
+                north, south = here - rows(v, r + 1), here - rows(v, r - 1)
+                rise = here - ahead(here)
+                images = []
+                for p in range(3):
+                    lift = rows(cross.at[6 + p], r) * rise
+                    image = rows(sums.at[p], r) * here + (lift - behind(lift))
+                    image = image + (rows(cross.at[p], r) * east + rows(cross.at[p], r - pitch) * west)
+                    image = image + (rows(cross.at[3 + p], r) * north + rows(cross.at[3 + p], r - 1) * south)
+                    images.append(image)
+                for p, change in enumerate(solve(r, images)):
+                    update[3 * i + p, pl.ds(r, SUB), :] = here - change
+            for p, change in enumerate(solve(r, [rows(source.at[p], r) for p in range(3)])):
+                update[3 * ITERS + p, pl.ds(r, SUB), :] = change
+        for start, r in grid.core():
+            for i in range(ITERS + 1):
+                here = [rows(update.at[3 * i + p], r) for p in range(3)]
+                images = []
+                for p in range(3):
+                    field = update.at[3 * i + p]
+                    lift = rows(cross.at[6 + p], r) * (here[p] - ahead(here[p]))
+                    image = lift - behind(lift)
+                    for q in range(3):
+                        image = image + rows(block.at[3 * p + q], r) * here[q]
+                    for base, shift in ((p, pitch), (3 + p, 1)):
+                        image = image + rows(cross.at[base], r) * (here[p] - rows(field, r + shift))
+                        image = image + rows(cross.at[base], r - shift) * (here[p] - rows(field, r - shift))
+                    images.append(image - rows(source.at[p], r) if i == ITERS else image)
+                for p, change in enumerate(solve(r, images)):
+                    swept[3 * i + p, pl.ds(start, SUB), :] = here[p] - change
+
     return kernel
 
 
 def finish(grid, devices):
-    pitch = grid.pitch
-
-    def kernel(gathered, v0, v1, v2, cross, inverse, sums, block, source, pressure_out, correction, pressure, update):
+    def kernel(gathered, v0, v1, v2, swept, pressure, correction):
         if devices <= 64:
             terms = [(gathered[i], jnp.zeros((1, LANES), jnp.float32)) for i in range(devices)]
             total = pair_tree(terms)
@@ -449,53 +523,18 @@
         moments = []
         for k in range(MOMENTS):
             high, low = (jnp.broadcast_to(t[:, k : k + 1], (SUB, LANES)) for t in total)
-            rest, _ = (jnp.broadcast_to(t[:, LOW + k : LOW + k + 1], (SUB, LANES)) for t in total)
+            rest = jnp.broadcast_to(total[0][:, LOW + k : LOW + k + 1], (SUB, LANES))
             moments.append(pair_add((high, low), (rest, jnp.zeros_like(rest))))
         weights = combination(moments)
-        for r in grid.chunks(2):
-            pressure[pl.ds(r, SUB), :] = (
+        for start, r in grid.core():
+            pressure[pl.ds(start, SUB), :] = (
                 weights[0] * rows(v0, r) + weights[1] * rows(v1, r) + weights[2] * rows(v2, r)
             )
-        for start, r in grid.core():
-            pressure_out[pl.ds(start, SUB), :] = rows(pressure, r)
-
-        def solve(r, defects):
-            return [
-                rows(inverse.at[3 * p], r) * defects[0]
-                + rows(inverse.at[3 * p + 1], r) * defects[1]
-                + rows(inverse.at[3 * p + 2], r) * defects[2]
-                for p in range(3)
-            ]
-
-        for r in grid.chunks(1):
-            here = rows(pressure, r)
-            east, west = here - rows(pressure, r + pitch), here - rows(pressure, r - pitch)
-            north, south = here - rows(pressure, r + 1), here - rows(pressure, r - 1)
-            rise = here - ahead(here)
-            defects = []
             for p in range(3):
-                lift = rows(cross.at[6 + p], r) * rise
-                image = rows(sums.at[p], r) * here + (lift - behind(lift))
-                image = image + (rows(cross.at[p], r) * east + rows(cross.at[p], r - pitch) * west)
-                image = image + (rows(cross.at[3 + p], r) * north + rows(cross.at[3 + p], r - 1) * south)
-                defects.append(rows(source.at[p], r) - image)
-            for p, change in enumerate(solve(r, defects)):
-                update[p, pl.ds(r, SUB), :] = here + change
-        for start, r in grid.core():
-            here = [rows(update.at[p], r) for p in range(3)]
-            defects = []
-            for p in range(3):
-                field = update.at[p]
-                lift = rows(cross.at[6 + p], r) * (here[p] - ahead(here[p]))
-                image = lift - behind(lift)
-                for q in range(3):
-                    image = image + rows(block.at[3 * p + q], r) * here[q]
-                for base, shift in ((p, pitch), (3 + p, 1)):
-                    image = image + rows(cross.at[base], r) * (here[p] - rows(field, r + shift))
-                    image = image + rows(cross.at[base], r - shift) * (here[p] - rows(field, r - shift))
-                defects.append(rows(source.at[p], r) - image)
-            for p, change in enumerate(solve(r, defects)):
-                correction[p, pl.ds(start, SUB), :] = here[p] + change
+                value = rows(swept.at[3 * ITERS + p], start)
+                for i, weight in enumerate(weights):
+                    value = value + weight * rows(swept.at[3 * i + p], start)
+                correction[p, pl.ds(start, SUB), :] = value
 
     return kernel
 
@@ -504,7 +543,11 @@
     devices = lax.axis_size(axis)
     up = [(i, (i + 1) % devices) for i in range(devices - 1)]
     down = [(j, i) for i, j in up]
-    return lax.ppermute(up_payload, axis, up), lax.ppermute(down_payload, axis, down)
+    return resident(lax.ppermute(up_payload, axis, up)), resident(lax.ppermute(down_payload, axis, down))
+
+
+def resident(value):
+    return pltpu.with_memory_space_constraint(value, pltpu.VMEM)
 
 
 def shards(rock_class, well_mask, perm_table, poro_table, accum, mobility, right_side):
@@ -517,25 +560,26 @@
     accum = accum.reshape((9,) + block)
     mobility = mobility.reshape((3,) + block)
     right = right_side.reshape((3,) + block)
-    a_rows, b_rows = (sum(A_PLANES) * ny, nz), (sum(B_PLANES) * ny, nz)
-    wide, near, a_up, a_down, b_up, b_down = call(
+    a_rows, b_rows = (sum(A_PLANES) * ny + SUB, nz), (sum(B_PLANES) * ny, nz)
+    loaded = [pltpu.with_memory_space_constraint(x, pltpu.HBM) for x in (rock, mask, accum, mobility, right)]
+    integers = pltpu.VMEM(block, jnp.int32)
+    wide, near, mobility, right, a_up, a_down = call(
         prepare(grid, perm_table.shape[0]),
         "prepare",
-        [(4,) + block, (10,) + block, a_rows, a_rows, b_rows, b_rows],
+        [(4,) + block, (10,) + block, (3,) + block, (3,) + block, a_rows, a_rows],
         perm_table,
         poro_table,
-        rock,
-        mask,
-        accum,
-        mobility,
-        right,
-        specs=[SMEM, SMEM] + [VMEM] * 5,
+        *loaded,
+        specs=[SMEM, SMEM] + [pl.BlockSpec(memory_space=pltpu.HBM)] * 5,
+        scratch=[integers, integers, pltpu.SemaphoreType.DMA((5,))],
     )
     a_before, a_after = shift_both(a_up, a_down, "gx")
+    y_rows = (y_count(grid), nz)
+    y_up, y_down, b_up, b_down = call(
+        pack(grid), "pack", [y_rows, y_rows, b_rows, b_rows], wide, near, mobility, right, a_before, a_after
+    )
+    y_before, y_after = shift_both(y_up, y_down, "gy")
     b_before, b_after = shift_both(b_up, b_down, "gx")
-    y_rows = (y_count(grid), nz)
-    y_up, y_down = call(pack(grid), "pack", [y_rows, y_rows], wide, near, mobility, right, a_before, a_after, b_before, b_after)
-    y_before, y_after = shift_both(y_up, y_down, "gy")
     scratch = pltpu.VMEM(extended, jnp.float32)
     partial, v0, v1, v2, perm = call(
         krylov(grid, devices),
@@ -548,12 +592,12 @@
         y_after,
         scratch=[scratch] * 5,
     )
-    gathered = lax.all_to_all(partial, ("gx", "gy"), 0, 0)
-    nine, three = (9,) + extended, (3,) + extended
-    cross, inverse, sums, blocks, source = call(
+    gathered = resident(lax.all_to_all(partial, ("gx", "gy"), 0, 0))
+    fields = lambda count: pltpu.VMEM((count,) + extended, jnp.float32)
+    (swept,) = call(
         precompute(grid),
         "precompute",
-        [nine, nine, three, nine, three],
+        [(3 * (ITERS + 1),) + block],
         near,
         mobility,
         right,
@@ -562,22 +606,13 @@
         y_before,
         y_after,
         perm,
-        scratch=[scratch, pltpu.VMEM(three, jnp.float32)],
-    )
-    pressure, correction = call(
-        finish(grid, devices),
-        "finish",
-        [block, (3,) + block],
-        gathered,
         v0,
         v1,
         v2,
-        cross,
-        inverse,
-        sums,
-        blocks,
-        source,
-        scratch=[scratch, pltpu.VMEM(three, jnp.float32)],
+        scratch=[fields(9), fields(9), fields(3), fields(9), fields(3), scratch, fields(3), fields(3 * (ITERS + 1))],
+    )
+    pressure, correction = call(
+        finish(grid, devices), "finish", [block, (3,) + block], gathered, v0, v1, v2, swept, resident=False
     )
     return pressure.reshape(nx, ny, nz), correction.reshape(3, nx, ny, nz)
 

time: 55.9 us -> 42.9 us (0.77)
  waiting for transfers between devices: 11.9 us -> 5.53 us
  Pallas kernels: 18 us -> 13.1 us
  local copies, waits for them, and re-layouts: 2.02 us -> 0.66 us
    pallas_call x5, Pallas kernels: 18 us -> 13.1 us  [call(): pl.pallas_call(kernel, name=name, out_shape=out, in_specs=specs or [VMEM]...]
    ppermute x3, waiting for transfers between devices: 8.14 us -> 4.18 us  [shift_both(): lax.ppermute(down_payload, axis, down)]
    all_to_all x1, waiting for transfers between devices: 2.27 us -> 0.01 us  [shards(): gathered = resident(lax.all_to_all(partial, ('gx', 'gy'), 0, 0))]
    unnamed x14 -> x4, local copies, waits for them, and re-layouts: 2.02 us -> 0.66 us
    ppermute x3, starting transfers between devices: 10.8 us -> 9.75 us  [shift_both(): lax.ppermute(up_payload, axis, up)]
    all_to_all x1, starting transfers between devices: 8.23 us -> 8.87 us  [shards(): gathered = resident(lax.all_to_all(partial, ('gx', 'gy'), 0, 0))]
  transfers between devices with their start and end apart: 7 -> 7, of which waited for: 4 -> 2; matrix products, arithmetic and copies ran while one was open for 0% -> 0% of each run, Pallas kernels for 9% -> 23%
where the time goes in v3:
time: 42.9 us; the launch traced here: 42.6 us
  starting transfers between devices  22.5 us (52%)
  Pallas kernels  13.1 us (31%)
  waiting for transfers between devices  5.53 us (13%)
  between operations  0.76 us (2%)
  local copies, waits for them, and re-layouts  0.66 us (2%)
    pallas_call x5, Pallas kernels, call(): pl.pallas_call(kernel, name=name, out_shape=out, in_specs=specs or [VMEM]...  13.1 us
    ppermute x3, starting transfers between devices, shift_both(): lax.ppermute(up_payload, axis, up)  9.75 us
    all_to_all x1, starting transfers between devices, shards(): gathered = resident(lax.all_to_all(partial, ('gx', 'gy'), 0, 0))  8.87 us
    ppermute x3, waiting for transfers between devices, shift_both(): lax.ppermute(down_payload, axis, down)  4.18 us
    ppermute x3, starting transfers between devices, shift_both(): lax.ppermute(down_payload, axis, down)  3.88 us
    ppermute x3, waiting for transfers between devices, shift_both(): lax.ppermute(up_payload, axis, up)  1.35 us
  transfers between devices with their start and end apart: 7, of which 2 were waited for; matrix products, arithmetic and copies ran while one was open for 0% of the time, Pallas kernels for 23%

profile of v3, /device:TPU:0, one launch (start us, length us, event | category | flops | bytes accessed | tf_op | source)
XLA Modules:
  0.0 42.6 jit_solution(13264204619566948560)
XLA Ops:
  0.6 0.0 copy-start
  0.6 0.0 copy-start.1
  0.7 0.6 %copy-done = f32[16]{0:T(128)S(1)} copy-done((f32[16]{0:T(128)S(1)}, f32[16]{0:T(128)}, u32[]{:S(2)}) %copy-start) | copy-done | bytes 88
  1.3 0.0 copy-done.1
  1.3 2.0 %prepare.1 = (f32[4,128,128]{2,1,0:T(8,128)S(1)}, f32[10,128,128]{2,1,0:T(8,128)S(1)}, f32[3,128,128]{2,1,0:T(8,128)S(1)}, f32[3,128,128]{2,1,0:T(8,128)S(1)}, f...) custom-call(f32[16]{0:T(128)S(1)} %copy-done, f32[16]{0:T(128)S(1)} %copy-done.1, s32[128,128]{1,0:T(8,128)} %bitcast.10, ...), custom_call_target="tpu_custom_call" | custom-call | tf_op jit(solution)/shard_map/prepare/pallas_call | solution.py:27
  3.3 5.0 %collective-permute-start = (f32[248,128]{1,0:T(8,128)S(1)}, f32[248,128]{1,0:T(8,128)S(1)}, u32[]{:S(2)}, u32[]{:S(2)}) collective-permute-start(f32[248,128]{1,0:T(8,128)S(1)} %get-tuple-element.20), channel_id=1, source_target_pairs={{0,8},{8,16},{16,24},{1,9},{9,17},{17,25},{2,10},{10,18},{18,26},{... | collective-permute-start | bytes 380936 | tf_op jit(solution)/shard_map/ppermute | solution.py:546
  8.3 1.3 %collective-permute-start.1 = (f32[248,128]{1,0:T(8,128)S(1)}, f32[248,128]{1,0:T(8,128)S(1)}, u32[]{:S(2)}, u32[]{:S(2)}) collective-permute-start(f32[248,128]{1,0:T(8,128)S(1)} %get-tuple-element.21), channel_id=1, source_target_pairs={{8,0},{16,8},{24,16},{9,1},{17,9},{25,17},{10,2},{18,10},{26,18},{... | collective-permute-start | bytes 380936 | tf_op jit(solution)/shard_map/ppermute | solution.py:546
  9.6 1.3 %collective-permute-done.a_before = f32[248,128]{1,0:T(8,128)S(1)} collective-permute-done((f32[248,128]{1,0:T(8,128)S(1)}, f32[248,128]{1,0:T(8,128)S(1)}, u32[]{:S(2)}, u32[]{:S(2)}) %collective-permute-start) | collective-permute-done | bytes 127008 | tf_op jit(solution)/shard_map/ppermute | solution.py:546
  10.9 4.2 %collective-permute-done.1.a_after = f32[248,128]{1,0:T(8,128)S(1)} collective-permute-done((f32[248,128]{1,0:T(8,128)S(1)}, f32[248,128]{1,0:T(8,128)S(1)}, u32[]{:S(2)}, u32[]{:S(2)}) %collective-permute-start.1) | collective-permute-done | bytes 127008 | tf_op jit(solution)/shard_map/ppermute | solution.py:546
  15.1 0.1 pack.1
  15.2 1.3 %collective-permute-start.2 = (f32[320,128]{1,0:T(8,128)S(1)}, f32[320,128]{1,0:T(8,128)S(1)}, u32[]{:S(2)}, u32[]{:S(2)}) collective-permute-start(f32[320,128]{1,0:T(8,128)S(1)} %get-tuple-element.25), channel_id=1, source_target_pairs={{0,1},{1,2},{2,3},{3,4},{4,5},{5,6},{6,7},{8,9},{9,10},{10,11},{11... | collective-permute-start | bytes 491528 | tf_op jit(solution)/shard_map/ppermute | solution.py:546
  16.5 1.3 %collective-permute-start.3 = (f32[320,128]{1,0:T(8,128)S(1)}, f32[320,128]{1,0:T(8,128)S(1)}, u32[]{:S(2)}, u32[]{:S(2)}) collective-permute-start(f32[320,128]{1,0:T(8,128)S(1)} %get-tuple-element.26), channel_id=1, source_target_pairs={{1,0},{2,1},{3,2},{4,3},{5,4},{6,5},{7,6},{9,8},{10,9},{11,10},{12... | collective-permute-start | bytes 491528 | tf_op jit(solution)/shard_map/ppermute | solution.py:546
  17.8 3.5 %collective-permute-start.4 = (f32[304,128]{1,0:T(8,128)S(1)}, f32[304,128]{1,0:T(8,128)S(1)}, u32[]{:S(2)}, u32[]{:S(2)}) collective-permute-start(f32[304,128]{1,0:T(8,128)S(1)} %get-tuple-element.31), channel_id=1, source_target_pairs={{0,8},{8,16},{16,24},{1,9},{9,17},{17,25},{2,10},{10,18},{18,26},{... | collective-permute-start | bytes 466952 | tf_op jit(solution)/shard_map/ppermute | solution.py:546
  21.3 1.3 %collective-permute-start.5 = (f32[304,128]{1,0:T(8,128)S(1)}, f32[304,128]{1,0:T(8,128)S(1)}, u32[]{:S(2)}, u32[]{:S(2)}) collective-permute-start(f32[304,128]{1,0:T(8,128)S(1)} %get-tuple-element.32), channel_id=1, source_target_pairs={{8,0},{16,8},{24,16},{9,1},{17,9},{25,17},{10,2},{18,10},{26,18},{... | collective-permute-start | bytes 466952 | tf_op jit(solution)/shard_map/ppermute | solution.py:546
  22.6 0.0 collective-permute-done.2.y_before
  22.7 0.0 collective-permute-done.3.y_after
  22.7 2.0 %krylov.1 = (f32[32,1,128]{2,1,0:T(1,128)}, f32[440,128]{1,0:T(8,128)S(1)}, f32[440,128]{1,0:T(8,128)S(1)}, f32[440,128]{1,0:T(8,128)S(1)}, f32[440,128]{1,0:T(8,128)S(1)}) custom-call(f32[4,128,128]{2,1,0:T(8,128)S(1)} %get-tuple-element.19.wide, f32[248,128]{1,0:T(8,128)S(1)} %collective-permute-done.a_before, ...), custom_call_target="tpu_custom_call" | custom-call | tf_op jit(solution)/shard_map/krylov/pallas_call | solution.py:27
  24.7 8.9 %all-to-all-start = ((f32[32,1,128]{2,1,0:T(1,128)}), f32[32,1,128]{2,1,0:T(1,128)S(1)}, u32[]{:S(2)}, u32[]{:S(2)}) async-start(f32[32,1,128]{2,1,0:T(1,128)} %get-tuple-element.27), calls=%async_computation | async-start | bytes 32768 | tf_op jit(solution)/shard_map/all_to_all | solution.py:595
  33.6 0.0 collective-permute-done.4.b_before
  33.6 0.0 collective-permute-done.5.b_after
  33.6 7.9 %precompute.1.swept = f32[12,128,128]{2,1,0:T(8,128)S(1)} custom-call(f32[10,128,128]{2,1,0:T(8,128)S(1)} %get-tuple-element.22.near, f32[3,128,128]{2,1,0:T(8,128)S(1)} %get-tuple-element.23.mobility, f32[3,128,128]{2,1,0:T(8,128)S(1)} %get-tuple-element.24.right, f32[304,128]{1,0:T(8,128)S(1)} %collective-permute-done.4.b_before, ...), custom_call_target="tpu_custom_call" | custom-call | tf_op jit(solution)/shard_map/precompute/pallas_call | solution.py:27
  41.5 0.0 all-to-all-done.gathered
  41.5 1.1 %finish.1 = (f32[128,128]{1,0:T(8,128)}, f32[3,128,128]{2,1,0:T(8,128)}) custom-call(f32[32,1,128]{2,1,0:T(1,128)S(1)} %all-to-all-done.gathered, f32[440,128]{1,0:T(8,128)S(1)} %get-tuple-element.28.v0, f32[440,128]{1,0:T(8,128)S(1)} %get-tuple-element.29.v1, f32[440,128]{1,0:T(8,128)S(1)} %get-tuple-element.30.v2, f32[12,128,128]{2,1,0:T(8,128)S(1)} %precompute.1.swept), custom_call_target="tpu_custom_call" | custom-call | tf_op jit(solution)/shard_map/finish/pallas_call | solution.py:27
Async XLA Ops:
  0.6 0.7 %copy-start = (f32[16]{0:T(128)S(1)}, f32[16]{0:T(128)}, u32[]{:S(2)}) copy-start(f32[16]{0:T(128)} %perm_table.1) | copy-start | bytes 196
  0.6 0.7 %copy-start.1 = (f32[16]{0:T(128)S(1)}, f32[16]{0:T(128)}, u32[]{:S(2)}) copy-start(f32[16]{0:T(128)} %poro_table.1) | copy-start | bytes 196
  3.3 7.6 %collective-permute-start = (f32[248,128]{1,0:T(8,128)S(1)}, f32[248,128]{1,0:T(8,128)S(1)}, u32[]{:S(2)}, u32[]{:S(2)}) collective-permute-start(f32[248,128]{1,0:T(8,128)S(1)} %get-tuple-element.20), channel_id=1, source_target_pairs={{0,8},{8,16},{16,24},{1,9},{9,17},{17,25},{2,10},{10,18},{18,26},{... | collective-permute-start | bytes 380936 | tf_op jit(solution)/shard_map/ppermute | solution.py:546
  8.3 6.8 %collective-permute-start.1 = (f32[248,128]{1,0:T(8,128)S(1)}, f32[248,128]{1,0:T(8,128)S(1)}, u32[]{:S(2)}, u32[]{:S(2)}) collective-permute-start(f32[248,128]{1,0:T(8,128)S(1)} %get-tuple-element.21), channel_id=1, source_target_pairs={{8,0},{16,8},{24,16},{9,1},{17,9},{25,17},{10,2},{18,10},{26,18},{... | collective-permute-start | bytes 380936 | tf_op jit(solution)/shard_map/ppermute | solution.py:546
  15.2 7.4 %collective-permute-start.2 = (f32[320,128]{1,0:T(8,128)S(1)}, f32[320,128]{1,0:T(8,128)S(1)}, u32[]{:S(2)}, u32[]{:S(2)}) collective-permute-start(f32[320,128]{1,0:T(8,128)S(1)} %get-tuple-element.25), channel_id=1, source_target_pairs={{0,1},{1,2},{2,3},{3,4},{4,5},{5,6},{6,7},{8,9},{9,10},{10,11},{11... | collective-permute-start | bytes 491528 | tf_op jit(solution)/shard_map/ppermute | solution.py:546
  16.5 6.1 %collective-permute-start.3 = (f32[320,128]{1,0:T(8,128)S(1)}, f32[320,128]{1,0:T(8,128)S(1)}, u32[]{:S(2)}, u32[]{:S(2)}) collective-permute-start(f32[320,128]{1,0:T(8,128)S(1)} %get-tuple-element.26), channel_id=1, source_target_pairs={{1,0},{2,1},{3,2},{4,3},{5,4},{6,5},{7,6},{9,8},{10,9},{11,10},{12... | collective-permute-start | bytes 491528 | tf_op jit(solution)/shard_map/ppermute | solution.py:546
  17.8 15.7 %collective-permute-start.4 = (f32[304,128]{1,0:T(8,128)S(1)}, f32[304,128]{1,0:T(8,128)S(1)}, u32[]{:S(2)}, u32[]{:S(2)}) collective-permute-start(f32[304,128]{1,0:T(8,128)S(1)} %get-tuple-element.31), channel_id=1, source_target_pairs={{0,8},{8,16},{16,24},{1,9},{9,17},{17,25},{2,10},{10,18},{18,26},{... | collective-permute-start | bytes 466952 | tf_op jit(solution)/shard_map/ppermute | solution.py:546
  21.3 12.2 %collective-permute-start.5 = (f32[304,128]{1,0:T(8,128)S(1)}, f32[304,128]{1,0:T(8,128)S(1)}, u32[]{:S(2)}, u32[]{:S(2)}) collective-permute-start(f32[304,128]{1,0:T(8,128)S(1)} %get-tuple-element.32), channel_id=1, source_target_pairs={{8,0},{16,8},{24,16},{9,1},{17,9},{25,17},{10,2},{18,10},{26,18},{... | collective-permute-start | bytes 466952 | tf_op jit(solution)/shard_map/ppermute | solution.py:546
  24.7 16.8 %all-to-all-start = ((f32[32,1,128]{2,1,0:T(1,128)}), f32[32,1,128]{2,1,0:T(1,128)S(1)}, u32[]{:S(2)}, u32[]{:S(2)}) async-start(f32[32,1,128]{2,1,0:T(1,128)} %get-tuple-element.27), calls=%async_computation | async-start | bytes 32768 | tf_op jit(solution)/shard_map/all_to_all | solution.py:595

commit v4 on v3

v4 whole, which is shorter than its diff:
```python
import jax
import jax.numpy as jnp
from jax import lax
from jax.experimental import pallas as pl
from jax.experimental.pallas import tpu as pltpu
from jax.sharding import PartitionSpec as P

ITERS = 3
FACE = (1.0, 1.0, 2.0)
WELL_FACTOR = 4.0
PERM_FLOOR = 0.005
W = 4
MOMENTS = 2 * ITERS
LOW = 8
STOP = 1e-12
SCOPED = 24 * 1024 * 1024
LANES = 128
SUB = 8

VMEM = pl.BlockSpec(memory_space=pltpu.VMEM)


def call(kernel, name, shapes, *operands, specs=None, out_specs=None, scratch=(), resident=True):
    kind = pltpu.VMEM if resident else jax.ShapeDtypeStruct
    out = [kind(shape, jnp.float32) for shape in shapes]
    return pl.pallas_call(
        kernel,
        name=name,
        out_shape=out,
        in_specs=specs or [VMEM] * len(operands),
        out_specs=out_specs or [VMEM] * len(out),
        scratch_shapes=list(scratch),
        compiler_params=pltpu.CompilerParams(vmem_limit_bytes=SCOPED),
    )(*operands)


def up8(count):
    return -(-count // SUB) * SUB


class Grid:
    def __init__(self, nx, ny, halo):
        self.nx, self.ny, self.halo = nx, ny, halo
        self.rows = nx * ny
        self.pitch = ny + 2 * halo
        self.front = up8(self.pitch)
        self.total = up8(self.front + (nx + 2 * halo) * self.pitch) + self.front + SUB

    def at(self, x, y):
        return self.front + (x + self.halo) * self.pitch + y + self.halo

    def chunks(self, depth):
        first = self.at(-depth, -depth)
        last = self.at(self.nx - 1 + depth, self.ny - 1 + depth)
        return range(first, last + 1, SUB)

    def core(self):
        for x in range(self.nx):
            for j in range(self.ny // SUB):
                yield x * self.ny + j * SUB, self.at(x, j * SUB)


def rows(ref, start, count=SUB):
    return ref[pl.ds(start, count), :]


def harmonic(left, right):
    return left * right / jnp.maximum(left + right, PERM_FLOOR)


def ahead(value):
    return pltpu.roll(value, LANES - 1, 1)


def behind(value):
    return pltpu.roll(value, 1, 1)


def open_face():
    lane = lax.broadcasted_iota(jnp.int32, (SUB, LANES), 1)
    return jnp.where(lane == LANES - 1, 0.0, 1.0)


def two_sum(a, b):
    total = a + b
    part = total - a
    return total, (a - (total - part)) + (b - part)


def split(a):
    scaled = a * 4097.0
    high = scaled - (scaled - a)
    return high, a - high


def two_prod(a, b, a_parts=None, b_parts=None):
    a_high, a_low = a_parts or split(a)
    b_high, b_low = b_parts or split(b)
    product = a * b
    return product, ((a_high * b_high - product) + a_high * b_low + a_low * b_high) + a_low * b_low


def pair_add(a, b):
    total, error = two_sum(a[0], b[0])
    error = error + (a[1] + b[1])
    high = total + error
    return high, error - (high - total)


def pair_mul(a, b):
    product, error = two_prod(a[0], b[0])
    error = error + (a[0] * b[1] + a[1] * b[0])
    high = product + error
    return high, error - (high - product)


def pair_tree(terms):
    terms = list(terms)
    while len(terms) > 1:
        joined = [pair_add(a, b) for a, b in zip(terms[::2], terms[1::2])]
        terms = joined + terms[len(terms) - len(terms) % 2 :]
    return terms[0]


def squares(poly):
    out = []
    for k in range(2 * len(poly) - 1):
        terms = []
        for i in range(max(0, k - len(poly) + 1), k // 2 + 1):
            high, low = two_prod(poly[i], poly[k - i])
            scale = 1.0 if 2 * i == k else 2.0
            terms.append((scale * high, scale * low))
        out.append(pair_tree(terms))
    return out


def norm(poly, moments, offset):
    return pair_tree(
        pair_mul(s, moments[k + offset]) for k, s in enumerate(squares(poly))
    )[0]


def combination(moments):
    one = jnp.ones_like(moments[0][0])
    zero = jnp.zeros_like(one)
    first = moments[0][0]
    residual, direction = [one], [one]
    result = [zero] * ITERS
    norm_now = first
    for iteration in range(ITERS):
        curvature = norm(direction, moments, 1)
        step = norm_now / curvature
        if iteration:
            step = jnp.where((norm_now > STOP * first) & (curvature > 0.0), step, 0.0)
        result = [r + step * d for r, d in zip(result, direction)] + result[len(direction) :]
        if iteration + 1 == ITERS:
            break
        residual = residual + [zero]
        residual = [residual[0]] + [r - step * d for r, d in zip(residual[1:], direction)]
        norm_next = norm(residual, moments, 0)
        mixing = norm_next / norm_now
        if iteration:
            mixing = jnp.where(norm_now > STOP * first, mixing, 0.0)
        direction = [r + mixing * d for r, d in zip(residual, direction + [zero])]
        norm_now = norm_next
    return result


A_PLANES = (W, W, W, W - 1)
B_PLANES = (2, 2, 2) + (1,) * 13


def is_even(axis):
    return lax.axis_index(axis) % 2 == 0


def send(even, first, second, start, high, low):
    count = high.shape[0]
    first[pl.ds(start, count), :] = jnp.where(even, high, low)
    second[pl.ds(start, count), :] = jnp.where(even, low, high)


def arrival(even, first, second, side):
    def read(start, count):
        a, b = rows(first, start, count), rows(second, start, count)
        return jnp.where(even, b, a) if side < 0 else jnp.where(even, a, b)

    return read


def send_planes(grid, even, fields, first, second):
    start = 0
    for ref, depth in fields:
        count = depth * grid.ny
        send(even, first, second, start, rows(ref, (grid.nx - depth) * grid.ny, count), rows(ref, 0, count))
        start += count
    return start


def prepare(grid, classes):
    nx, ny = grid.nx, grid.ny

    def kernel(
        perm_in, poro_in, rock_in, mask_in, accum_in, mobility_in, right_in,
        wide, near, mobility, right, first, second, rock, mask, perm_table, poro_table, arrived,
    ):
        copies = [
            pltpu.make_async_copy(source, target, arrived.at[i])
            for i, (source, target) in enumerate(
                (
                    (perm_in, perm_table),
                    (poro_in, poro_table),
                    (rock_in, rock),
                    (mask_in, mask),
                    (mobility_in, mobility),
                    (right_in, right),
                    (accum_in, near.at[pl.ds(0, 9)]),
                )
            )
        ]
        for copy in copies:
            copy.start()
        for copy in copies[:3]:
            copy.wait()
        for r in range(0, grid.rows, SUB):
            kind = rows(rock, r)
            perm = jnp.zeros((SUB, LANES), jnp.float32)
            poro = perm
            for k in range(classes):
                hit = kind == k
                perm = jnp.where(hit, perm_table[k], perm)
                poro = jnp.where(hit, poro_table[k], poro)
            wide[1, pl.ds(r, SUB), :] = perm
            wide[3, pl.ds(r, SUB), :] = poro
        for copy in copies[3:6]:
            copy.wait()
        for r in range(0, grid.rows, SUB):
            near[9, pl.ds(r, SUB), :] = (WELL_FACTOR * rows(wide.at[1], r)) * rows(mask, r).astype(jnp.float32)
            for out, fields in ((0, right), (2, mobility)):
                wide[out, pl.ds(r, SUB), :] = rows(fields.at[0], r) + rows(fields.at[1], r) + rows(fields.at[2], r)
        copies[6].wait()
        for r in range(0, grid.rows, SUB):
            poro = rows(wide.at[3], r)
            parts = []
            for k in range(9):
                part = poro * rows(near.at[k], r)
                near[k, pl.ds(r, SUB), :] = part
                parts.append(part)
            stored = ((parts[0] + parts[1]) + (parts[2] + parts[3])) + ((parts[4] + parts[5]) + (parts[6] + parts[7])) + parts[8]
            wide[3, pl.ds(r, SUB), :] = stored + rows(near.at[9], r) * rows(wide.at[2], r)
        even = is_even("gx")
        fields = [(wide.at[f], depth) for f, depth in enumerate(A_PLANES)]
        start = send_planes(grid, even, fields, first, second)
        for p in range(3):
            for k, y in enumerate((0, ny - 1)):
                high = rows(mobility.at[p], (nx - 1) * ny + y, 1)
                send(even, first, second, start + 2 * p + k, high, rows(mobility.at[p], y, 1))
        blank = jnp.zeros((2, LANES), jnp.float32)
        send(even, first, second, start + 6, blank, blank)

    return kernel


def side_rows(grid):
    out = []
    for field in range(4):
        reach = W if field < 3 else W - 1
        for distance in range(1, reach):
            out.append((field, distance, reach - distance))
    return out


def received(grid, planes, field, distance, side):
    start = sum(planes[:field])
    index = planes[field] - distance if side < 0 else distance - 1
    return (start + index) * grid.ny


def corner_rows(grid):
    out = []
    for side in (-1, 1):
        for field, distance, depth in side_rows(grid):
            for k in range(depth):
                out.append((0, field, side, distance, k, depth))
        for p in range(3):
            out.append((1, p, side, 1, 0, 1))
    return out


def edge_rows():
    out = []
    for field in range(4):
        reach = W if field < 3 else W - 1
        out += [(0, field, k, reach) for k in range(reach)]
    for p in range(3):
        out += [(1, p, k, 2) for k in range(2)]
    out += [(1, 3 + f, 0, 1) for f in range(13)]
    return out


def y_count(grid):
    count = len(edge_rows()) * grid.nx + len(corner_rows(grid))
    return -(-count // SUB) * SUB


def pack(grid):
    nx, ny = grid.nx, grid.ny

    def kernel(wide, near, mobility, right, a_first, a_second, first, second, b_first, b_second):
        later = [mobility.at[p] for p in range(3)] + [near.at[k] for k in range(9)]
        later += [right.at[p] for p in range(3)] + [near.at[9]]
        even_x, even_y = is_even("gx"), is_even("gy")
        sides = {side: arrival(even_x, a_first, a_second, side) for side in (-1, 1)}
        start = 0
        for group, field, k, depth in edge_rows():
            ref = later[field] if group else wide.at[field]
            high = ref[pl.ds(ny - depth + k, nx, stride=ny), :]
            send(even_y, first, second, start, high, ref[pl.ds(k, nx, stride=ny), :])
            start += nx
        for group, field, side, distance, k, depth in corner_rows(grid):
            if group:
                base = sum(A_PLANES) * ny + 2 * field
                high, low = base + 1, base
            else:
                base = received(grid, A_PLANES, field, distance, side)
                high, low = base + ny - depth + k, base + k
            send(even_y, first, second, start, sides[side](high, 1), sides[side](low, 1))
            start += 1
        left = y_count(grid) - start
        if left:
            blank = jnp.zeros((left, LANES), jnp.float32)
            send(even_y, first, second, start, blank, blank)
        send_planes(grid, even_x, list(zip(later, B_PLANES)), b_first, b_second)

    return kernel


def spread(grid, wanted, target, local, x_first, x_second, y_first, y_second, columns):
    nx, ny = grid.nx, grid.ny
    planes = B_PLANES if wanted else A_PLANES
    sides_x = {side: arrival(is_even("gx"), x_first, x_second, side) for side in (-1, 1)}
    sides_y = {side: arrival(is_even("gy"), y_first, y_second, side) for side in (-1, 1)}
    column = lax.axis_index("gy")
    open_y = {-1: column > 0, 1: column < columns - 1}

    def from_y(field, side, start, count):
        value = sides_y[side](start, count)
        return jnp.where(open_y[side], value, 0.0) if (wanted, field) == (0, 1) else value

    for field, depth in enumerate(planes):
        ref = target(field)
        source = local(field)
        for x in range(nx):
            ref[pl.ds(grid.at(x, 0), ny), :] = rows(source, x * ny, ny)
        for distance in range(1, depth + 1):
            for side, x in ((-1, -distance), (1, nx - 1 + distance)):
                ref[pl.ds(grid.at(x, 0), ny), :] = sides_x[side](received(grid, planes, field, distance, side), ny)
    start = 0
    for group, field, k, depth in edge_rows():
        if group == wanted:
            ref = target(field)
            for side, y in ((-1, k - depth), (1, ny + k)):
                ref[pl.ds(grid.at(0, y), nx, stride=grid.pitch), :] = from_y(field, side, start, nx)
        start += nx
    for group, field, side_x, distance, k, depth in corner_rows(grid):
        if group == wanted:
            ref = target(field)
            x = -distance if side_x < 0 else nx - 1 + distance
            for side, y in ((-1, k - depth), (1, ny + k)):
                ref[pl.ds(grid.at(x, y), 1), :] = from_y(field, side, start, 1)
        start += 1


def krylov(grid, tight, devices, columns):
    pitch = grid.pitch

    def kernel(
        wide, a_first, a_second, y_first, y_second,
        partial, t0, t1, t2, t_perm, v0, v1, v2, perm, summed, storage, cross_x, cross_y, cross_z, cross_b,
    ):
        fields = (v0, perm, summed, storage)
        spread(grid, 0, lambda f: fields[f], lambda f: wide.at[f], a_first, a_second, y_first, y_second, columns)
        inside = open_face()
        for r in range(grid.at(-W, -W), grid.at(grid.nx - 1 + W, grid.ny), SUB):
            k, s = rows(perm, r), rows(summed, r)
            for ref, shift, scale in ((cross_x, pitch, FACE[0]), (cross_y, 1, FACE[1])):
                ref[pl.ds(r, SUB), :] = scale * harmonic(k, rows(perm, r + shift)) * (s + rows(summed, r + shift))
            upper = (FACE[2] * inside) * harmonic(k, ahead(k)) * (s + ahead(s))
            cross_z[pl.ds(r, SUB), :] = upper
            cross_b[pl.ds(r, SUB), :] = behind(upper)

        def operate(v, r):
            here = rows(v, r)
            out = rows(storage, r) * here
            out = out + rows(cross_z, r) * (here - ahead(here))
            out = out + rows(cross_b, r) * (here - behind(here))
            for ref, shift in ((cross_x, pitch), (cross_y, 1)):
                out = out + rows(ref, r) * (here - rows(v, r + shift))
                out = out + rows(ref, r - shift) * (here - rows(v, r - shift))
            return out

        for depth, source, target in ((W - 1, v0, v1), (W - 2, v1, v2)):
            for r in grid.chunks(depth):
                target[pl.ds(r, SUB), :] = operate(source, r)
        for source, target in ((v0, t0), (v1, t1), (v2, t2), (perm, t_perm)):
            for x in range(-2, grid.nx + 2):
                target[pl.ds(tight.at(x, -2), tight.pitch), :] = rows(source, grid.at(x, -2), tight.pitch)
        zero = jnp.zeros((SUB, LANES), jnp.float32)
        sums = [(zero, zero)] * MOMENTS
        for _, r in grid.core():
            basis = [rows(v0, r), rows(v1, r), rows(v2, r), operate(v2, r)]
            parts = [split(b) for b in basis]
            for k in range(MOMENTS):
                i, j = k // 2, k - k // 2
                product, error = two_prod(basis[i], basis[j], parts[i], parts[j])
                total, lost = two_sum(sums[k][0], product)
                sums[k] = (total, sums[k][1] + (lost + error))
        for shift in (4, 2, 1):
            sums = [pair_add(s, tuple(pltpu.roll(part, shift, 0) for part in s)) for s in sums]
        sub = lax.broadcasted_iota(jnp.int32, (SUB, LANES), 0)
        lane = lax.broadcasted_iota(jnp.int32, (SUB, LANES), 1)
        high, low = zero, zero
        for k, s in enumerate(sums):
            high = jnp.where(sub == k, s[0], high)
            low = jnp.where(sub == k, s[1], low)
        pair = (high, low)
        shift = LANES // 2
        while shift:
            pair = pair_add(pair, tuple(pltpu.roll(part, shift, 1) for part in pair))
            shift //= 2
        picked = jnp.where(lane == sub, pair[0], 0.0) + jnp.where(lane == sub + LOW, pair[1], 0.0)
        for shift in (4, 2, 1):
            picked = picked + pltpu.roll(picked, shift, 0)
        row = picked[0:1]

        def put(i, carry):
            partial[i] = row
            return carry

        lax.fori_loop(0, devices, put, 0, unroll=devices <= 64)

    return kernel


class Region:
    def __init__(self, tight):
        self.first = tight.at(-1, -1)
        self.chunks = tight.chunks(1)
        self.length = len(self.chunks) * SUB
        self.lead = up8(tight.pitch)

    def near(self, ref, field, r):
        return ref.at[field, pl.ds(r - self.first, SUB)]

    def face(self, ref, field, r):
        return ref.at[field, pl.ds(r - self.first + self.lead, SUB)]


def precompute(tight, columns):
    pitch = tight.pitch
    region = Region(tight)

    def kernel(
        near, mobility, right, b_first, b_second, y_first, y_second, perm, v0, v1, v2,
        swept, cross, cross_b, inverse, source, mobile, block, well, ends, update,
    ):
        later = [mobile.at[p] for p in range(3)] + [block.at[k] for k in range(9)]
        later += [ends.at[p] for p in range(3)] + [well]
        local = [mobility.at[p] for p in range(3)] + [near.at[k] for k in range(9)]
        local += [right.at[p] for p in range(3)] + [near.at[9]]
        spread(tight, 1, lambda f: later[f], lambda f: local[f], b_first, b_second, y_first, y_second, columns)
        inside = open_face()
        for r in range(region.first - region.lead, region.first + region.length, SUB):
            k = rows(perm, r)
            along_x = FACE[0] * harmonic(k, rows(perm, r + pitch))
            along_y = FACE[1] * harmonic(k, rows(perm, r + 1))
            whole = r >= region.first
            along_z = (FACE[2] * inside) * harmonic(k, ahead(k)) if whole else None
            for p in range(3):
                m = rows(mobile.at[p], r)
                region.face(cross, p, r)[...] = along_x * (m + rows(mobile.at[p], r + pitch))
                region.face(cross, 3 + p, r)[...] = along_y * (m + rows(mobile.at[p], r + 1))
                if whole:
                    upper = along_z * (m + ahead(m))
                    region.face(cross, 6 + p, r)[...] = upper
                    region.near(cross_b, p, r)[...] = behind(upper)
        for r in region.chunks:
            drain = rows(well, r)
            blocks = [[rows(block.at[3 * p + q], r) for q in range(3)] for p in range(3)]
            for p in range(3):
                flow = region.face(cross, p, r)[...] + region.face(cross, p, r - pitch)[...]
                flow = flow + (region.face(cross, 3 + p, r)[...] + region.face(cross, 3 + p, r - 1)[...])
                flow = flow + (region.face(cross, 6 + p, r)[...] + region.near(cross_b, p, r)[...])
                blocks[p][p] = blocks[p][p] + (flow + drain * rows(mobile.at[p], r))
                region.near(source, p, r)[...] = rows(ends.at[p], r)

            def cofactor(i, j):
                a, b, c, d = (i + 1) % 3, (i + 2) % 3, (j + 1) % 3, (j + 2) % 3
                return blocks[a][c] * blocks[b][d] - blocks[a][d] * blocks[b][c]

            adjugate = [[cofactor(j, i) for j in range(3)] for i in range(3)]
            determinant = blocks[0][0] * adjugate[0][0] + blocks[0][1] * adjugate[1][0] + blocks[0][2] * adjugate[2][0]
            scale = 1.0 / jnp.where(determinant == 0.0, 1.0, determinant)
            for i in range(3):
                for j in range(3):
                    region.near(inverse, 3 * i + j, r)[...] = adjugate[i][j] * scale

        def solve(r, sums):
            return [
                region.near(inverse, 3 * p, r)[...] * sums[0]
                + region.near(inverse, 3 * p + 1, r)[...] * sums[1]
                + region.near(inverse, 3 * p + 2, r)[...] * sums[2]
                for p in range(3)
            ]

        def neighbours(p, read, r, here, above, below):
            total = region.face(cross, 6 + p, r)[...] * above + region.near(cross_b, p, r)[...] * below
            for base, shift in ((p, pitch), (3 + p, 1)):
                total = total + (
                    region.face(cross, base, r)[...] * read(r + shift)
                    + region.face(cross, base, r - shift)[...] * read(r - shift)
                )
            return total

        for r in region.chunks:
            for i, v in enumerate((v0, v1, v2)):
                here = rows(v, r)
                above, below = ahead(here), behind(here)
                read = lambda at, v=v: rows(v, at)
                sums = [neighbours(p, read, r, here, above, below) for p in range(3)]
                for p, value in enumerate(solve(r, sums)):
                    region.near(update, 3 * i + p, r)[...] = value
            sums = [region.near(source, p, r)[...] for p in range(3)]
            for p, value in enumerate(solve(r, sums)):
                region.near(update, 3 * ITERS + p, r)[...] = value
        for start, r in tight.core():
            for i in range(ITERS + 1):
                sums = []
                for p in range(3):
                    read = lambda at, f=3 * i + p: region.near(update, f, at)[...]
                    here = read(r)
                    total = neighbours(p, read, r, here, ahead(here), behind(here))
                    sums.append(total + region.near(source, p, r)[...] if i == ITERS else total)
                for p, value in enumerate(solve(r, sums)):
                    swept[3 * i + p, pl.ds(start, SUB), :] = value

    return kernel


def finish(tight, devices):
    half = tight.nx // 2 * tight.ny

    def kernel(gathered, v0, v1, v2, swept, pressure_out, correction_out, pressure, result, sent):
        if devices <= 64:
            terms = [(gathered[i], jnp.zeros((1, LANES), jnp.float32)) for i in range(devices)]
            total = pair_tree(terms)
        else:
            zero = jnp.zeros((1, LANES), jnp.float32)
            total = lax.fori_loop(0, devices, lambda i, t: pair_add(t, (gathered[i], zero)), (zero, zero))
        moments = []
        for k in range(MOMENTS):
            high, low = (jnp.broadcast_to(t[:, k : k + 1], (SUB, LANES)) for t in total)
            rest = jnp.broadcast_to(total[0][:, LOW + k : LOW + k + 1], (SUB, LANES))
            moments.append(pair_add((high, low), (rest, jnp.zeros_like(rest))))
        weights = combination(moments)
        copies = []

        def ship(source, target, first, count):
            copy = pltpu.make_async_copy(source.at[pl.ds(first, count)], target.at[pl.ds(first, count)], sent.at[len(copies)])
            copy.start()
            copies.append(copy)

        done = 0
        for start, r in tight.core():
            pressure[pl.ds(start, SUB), :] = (
                weights[0] * rows(v0, r) + weights[1] * rows(v1, r) + weights[2] * rows(v2, r)
            )
            for p in range(3):
                value = rows(swept.at[3 * ITERS + p], start)
                for i, weight in enumerate(weights):
                    value = value + weight * rows(swept.at[3 * i + p], start)
                result[p, pl.ds(start, SUB), :] = value
            if start + SUB in (half, tight.rows):
                count = start + SUB - done
                ship(pressure, pressure_out, done, count)
                for p in range(3):
                    ship(result.at[p], correction_out.at[p], done, count)
                done = start + SUB
        for copy in copies:
            copy.wait()

    return kernel


def swap(first, second, axis, ring):
    devices = lax.axis_size(axis)
    even = [(i, i + 1) for i in range(0, devices - 1, 2)]
    odd = [(i, i + 1) for i in range(1, devices - 1, 2)]
    if ring and devices % 2 == 0 and devices > 2:
        odd.append((devices - 1, 0))
    both = lambda pairs: pairs + [(j, i) for i, j in pairs]
    return resident(lax.ppermute(first, axis, both(even))), resident(lax.ppermute(second, axis, both(odd)))


def resident(value):
    return pltpu.with_memory_space_constraint(value, pltpu.VMEM)


def shards(rock_class, well_mask, perm_table, poro_table, accum, mobility, right_side):
    nx, ny, nz = rock_class.shape
    grid, tight = Grid(nx, ny, W), Grid(nx, ny, 2)
    region = Region(tight)
    columns = lax.axis_size("gy")
    devices = lax.axis_size("gx") * columns
    block = (grid.rows, nz)
    operands = [
        perm_table,
        poro_table,
        rock_class.reshape(block),
        well_mask.reshape(block),
        accum.reshape((9,) + block),
        mobility.reshape((3,) + block),
        right_side.reshape((3,) + block),
    ]
    hbm = pl.BlockSpec(memory_space=pltpu.HBM)
    integers = pltpu.VMEM(block, jnp.int32)
    table = pltpu.SMEM(perm_table.shape, jnp.float32)
    a_rows, b_rows = (sum(A_PLANES) * ny + SUB, nz), (sum(B_PLANES) * ny, nz)
    wide, near, mobility, right, a_first, a_second = call(
        prepare(grid, perm_table.shape[0]),
        "prepare",
        [(4,) + block, (10,) + block, (3,) + block, (3,) + block, a_rows, a_rows],
        *[pltpu.with_memory_space_constraint(x, pltpu.HBM) for x in operands],
        specs=[hbm] * len(operands),
        scratch=[integers, integers, table, table, pltpu.SemaphoreType.DMA((len(operands),))],
    )
    a_first, a_second = swap(a_first, a_second, "gx", False)
    y_rows = (y_count(grid), nz)
    y_first, y_second, b_first, b_second = call(
        pack(grid), "pack", [y_rows, y_rows, b_rows, b_rows], wide, near, mobility, right, a_first, a_second
    )
    y_first, y_second = swap(y_first, y_second, "gy", True)
    b_first, b_second = swap(b_first, b_second, "gx", False)
    field = lambda rows, *count: pltpu.VMEM(count + (rows, nz), jnp.float32)
    partial, v0, v1, v2, perm = call(
        krylov(grid, tight, devices, columns),
        "krylov",
        [(devices, 1, nz)] + [(tight.total, nz)] * 4,
        wide,
        a_first,
        a_second,
        y_first,
        y_second,
        scratch=[field(grid.total)] * 10,
    )
    gathered = resident(lax.all_to_all(partial, ("gx", "gy"), 0, 0))
    (swept,) = call(
        precompute(tight, columns),
        "precompute",
        [(3 * (ITERS + 1),) + block],
        near,
        mobility,
        right,
        b_first,
        b_second,
        y_first,
        y_second,
        perm,
        v0,
        v1,
        v2,
        scratch=[
            field(region.lead + region.length, 9),
            field(region.length, 3),
            field(region.length, 9),
            field(region.length, 3),
            field(tight.total, 3),
            field(tight.total, 9),
            field(tight.total),
            field(tight.total, 3),
            field(region.length, 3 * (ITERS + 1)),
        ],
    )
    pressure, correction = call(
        finish(tight, devices),
        "finish",
        [block, (3,) + block],
        gathered,
        v0,
        v1,
        v2,
        swept,
        out_specs=[hbm, hbm],
        scratch=[field(grid.rows), field(grid.rows, 3), pltpu.SemaphoreType.DMA((8,))],
        resident=False,
    )
    return pressure.reshape(nx, ny, nz), correction.reshape(3, nx, ny, nz)


def solution(mesh):
    return jax.shard_map(
        shards,
        mesh=mesh,
        in_specs=(
            P("gx", "gy", None),
            P("gx", "gy", None),
            P(),
            P(),
            P(None, None, "gx", "gy", None),
            P(None, "gx", "gy", None),
            P(None, "gx", "gy", None),
        ),
        out_specs=(P("gx", "gy", None), P(None, "gx", "gy", None)),
        check_vma=False,
    )
```

time: 42.9 us -> 33.7 us (0.79)
  Pallas kernels: 13.1 us -> 7.17 us
  starting transfers between devices: 22.5 us -> 18.2 us
  waiting for transfers between devices: 5.53 us -> 7.41 us
  local copies, waits for them, and re-layouts: 0.66 us -> 0 us
    pallas_call x5, Pallas kernels: 13.1 us -> 7.17 us  [call(): pl.pallas_call(kernel, name=name, out_shape=out, in_specs=specs or [VMEM]...]
    all_to_all x1, waiting for transfers between devices: 0.01 us -> 4.65 us  [shards(): gathered = resident(lax.all_to_all(partial, ('gx', 'gy'), 0, 0))]
    ppermute x6, waiting for transfers between devices: 5.53 us -> 2.76 us  [the longest x3 2.75 us: swap(): lax.ppermute(first, axis, both(even))]
    all_to_all x1, starting transfers between devices: 8.87 us -> 6.42 us  [shards(): gathered = resident(lax.all_to_all(partial, ('gx', 'gy'), 0, 0))]
    ppermute x6, starting transfers between devices: 13.6 us -> 11.8 us  [the longest x3 7.78 us: swap(): lax.ppermute(first, axis, both(even))]
    unnamed x4 -> x0, local copies, waits for them, and re-layouts: 0.66 us -> none
  transfers between devices with their start and end apart: 7 -> 7, of which waited for: 2 -> 2; matrix products, arithmetic and copies ran while one was open for 0% -> 0% of each run, Pallas kernels for 23% -> 13%
where the time goes in v4:
time: 33.7 us; the launch traced here: 33.5 us
  starting transfers between devices  18.2 us (54%)
  waiting for transfers between devices  7.41 us (22%)
  Pallas kernels  7.17 us (21%)
  between operations  0.72 us (2%)
    ppermute x3, starting transfers between devices, swap(): lax.ppermute(first, axis, both(even))  7.78 us
    pallas_call x5, Pallas kernels, call(): pl.pallas_call(kernel, name=name, out_shape=out, in_specs=specs or [VMEM]...  7.17 us
    all_to_all x1, starting transfers between devices, shards(): gathered = resident(lax.all_to_all(partial, ('gx', 'gy'), 0, 0))  6.42 us
    all_to_all x1, waiting for transfers between devices, shards(): gathered = resident(lax.all_to_all(partial, ('gx', 'gy'), 0, 0))  4.65 us
    ppermute x3, starting transfers between devices, swap(): lax.ppermute(second, axis, both(odd))  4.03 us
    ppermute x3, waiting for transfers between devices, swap(): lax.ppermute(first, axis, both(even))  2.75 us
  transfers between devices with their start and end apart: 7, of which 2 were waited for; matrix products, arithmetic and copies ran while one was open for 0% of the time, Pallas kernels for 13%

profile of v4, /device:TPU:0, one launch (start us, length us, event | category | flops | bytes accessed | tf_op | source)
XLA Modules:
  0.0 33.5 jit_solution(4265546440676075300)
XLA Ops:
  0.6 1.5 %prepare.1 = (f32[4,128,128]{2,1,0:T(8,128)S(1)}, f32[10,128,128]{2,1,0:T(8,128)S(1)}, f32[3,128,128]{2,1,0:T(8,128)S(1)}, f32[3,128,128]{2,1,0:T(8,128)S(1)}, f...) custom-call(f32[16]{0:T(128)} %perm_in.1, f32[16]{0:T(128)} %poro_in.1, s32[128,128]{1,0:T(8,128)} %bitcast.10, ...), custom_call_target="tpu_custom_call" | custom-call | tf_op jit(solution)/shard_map/prepare/pallas_call | solution.py:26
  2.1 3.1 %collective-permute-start = (f32[248,128]{1,0:T(8,128)S(1)}, f32[248,128]{1,0:T(8,128)S(1)}, u32[]{:S(2)}, u32[]{:S(2)}) collective-permute-start(f32[248,128]{1,0:T(8,128)S(1)} %get-tuple-element.20), channel_id=1, source_target_pairs={{0,8},{16,24},{8,0},{24,16},{1,9},{17,25},{9,1},{25,17},{2,10},{18... | collective-permute-start | bytes 380936 | tf_op jit(solution)/shard_map/ppermute | solution.py:602
  5.2 0.7 %collective-permute-start.1 = (f32[248,128]{1,0:T(8,128)S(1)}, f32[248,128]{1,0:T(8,128)S(1)}, u32[]{:S(2)}, u32[]{:S(2)}) collective-permute-start(f32[248,128]{1,0:T(8,128)S(1)} %get-tuple-element.21), channel_id=1, source_target_pairs={{8,16},{16,8},{9,17},{17,9},{10,18},{18,10},{11,19},{19,11},{12,20... | collective-permute-start | bytes 380936 | tf_op jit(solution)/shard_map/ppermute | solution.py:602
  5.9 2.7 %collective-permute-done.a_first = f32[248,128]{1,0:T(8,128)S(1)} collective-permute-done((f32[248,128]{1,0:T(8,128)S(1)}, f32[248,128]{1,0:T(8,128)S(1)}, u32[]{:S(2)}, u32[]{:S(2)}) %collective-permute-start) | collective-permute-done | bytes 127008 | tf_op jit(solution)/shard_map/ppermute | solution.py:602
  8.6 0.0 collective-permute-done.1.a_second
  8.7 0.2 pack.1
  8.8 0.1 collective-permute-start.2
  8.9 2.7 %collective-permute-start.3 = (f32[320,128]{1,0:T(8,128)S(1)}, f32[320,128]{1,0:T(8,128)S(1)}, u32[]{:S(2)}, u32[]{:S(2)}) collective-permute-start(f32[320,128]{1,0:T(8,128)S(1)} %get-tuple-element.26), channel_id=1, source_target_pairs={{1,2},{3,4},{5,6},{7,0},{2,1},{4,3},{6,5},{0,7},{9,10},{11,12},{13... | collective-permute-start | bytes 491528 | tf_op jit(solution)/shard_map/ppermute | solution.py:602
  11.6 4.6 %collective-permute-start.4 = (f32[304,128]{1,0:T(8,128)S(1)}, f32[304,128]{1,0:T(8,128)S(1)}, u32[]{:S(2)}, u32[]{:S(2)}) collective-permute-start(f32[304,128]{1,0:T(8,128)S(1)} %get-tuple-element.31), channel_id=1, source_target_pairs={{0,8},{16,24},{8,0},{24,16},{1,9},{17,25},{9,1},{25,17},{2,10},{18... | collective-permute-start | bytes 466952 | tf_op jit(solution)/shard_map/ppermute | solution.py:602
  16.2 0.7 %collective-permute-start.5 = (f32[304,128]{1,0:T(8,128)S(1)}, f32[304,128]{1,0:T(8,128)S(1)}, u32[]{:S(2)}, u32[]{:S(2)}) collective-permute-start(f32[304,128]{1,0:T(8,128)S(1)} %get-tuple-element.32), channel_id=1, source_target_pairs={{8,16},{16,8},{9,17},{17,9},{10,18},{18,10},{11,19},{19,11},{12,20... | collective-permute-start | bytes 466952 | tf_op jit(solution)/shard_map/ppermute | solution.py:602
  16.9 0.0 collective-permute-done.2.y_first
  16.9 0.0 collective-permute-done.3.y_second
  16.9 2.0 %krylov.1 = (f32[32,1,128]{2,1,0:T(1,128)}, f32[296,128]{1,0:T(8,128)S(1)}, f32[296,128]{1,0:T(8,128)S(1)}, f32[296,128]{1,0:T(8,128)S(1)}, f32[296,128]{1,0:T(8,128)S(1)}) custom-call(f32[4,128,128]{2,1,0:T(8,128)S(1)} %get-tuple-element.19.wide, f32[248,128]{1,0:T(8,128)S(1)} %collective-permute-done.a_first, ...), custom_call_target="tpu_custom_call" | custom-call | tf_op jit(solution)/shard_map/krylov/pallas_call | solution.py:26
  18.9 6.4 %all-to-all-start = ((f32[32,1,128]{2,1,0:T(1,128)}), f32[32,1,128]{2,1,0:T(1,128)S(1)}, u32[]{:S(2)}, u32[]{:S(2)}) async-start(f32[32,1,128]{2,1,0:T(1,128)} %get-tuple-element.27), calls=%async_computation | async-start | bytes 32768 | tf_op jit(solution)/shard_map/all_to_all | solution.py:656
  25.3 0.0 collective-permute-done.4.b_first
  25.3 0.0 collective-permute-done.5.b_second
  25.3 2.4 %precompute.1.swept = f32[12,128,128]{2,1,0:T(8,128)S(1)} custom-call(f32[10,128,128]{2,1,0:T(8,128)S(1)} %get-tuple-element.22.near, f32[3,128,128]{2,1,0:T(8,128)S(1)} %get-tuple-element.23.mobility, f32[3,128,128]{2,1,0:T(8,128)S(1)} %get-tuple-element.24.right, f32[304,128]{1,0:T(8,128)S(1)} %collective-permute-done.4.b_first, ...), custom_call_target="tpu_custom_call" | custom-call | tf_op jit(solution)/shard_map/precompute/pallas_call | solution.py:26
  27.8 4.6 %all-to-all-done.gathered = f32[32,1,128]{2,1,0:T(1,128)S(1)} async-done(((f32[32,1,128]{2,1,0:T(1,128)}), f32[32,1,128]{2,1,0:T(1,128)S(1)}, u32[]{:S(2)}, u32[]{:S(2)}) %all-to-all-start) | async-done | bytes 16416 | tf_op jit(solution)/shard_map/all_to_all | solution.py:656
  32.4 1.1 %finish.1 = (f32[128,128]{1,0:T(8,128)}, f32[3,128,128]{2,1,0:T(8,128)}) custom-call(f32[32,1,128]{2,1,0:T(1,128)S(1)} %all-to-all-done.gathered, f32[296,128]{1,0:T(8,128)S(1)} %get-tuple-element.28.v0, f32[296,128]{1,0:T(8,128)S(1)} %get-tuple-element.29.v1, f32[296,128]{1,0:T(8,128)S(1)} %get-tuple-element.30.v2, f32[12,128,128]{2,1,0:T(8,128)S(1)} %precompute.1.swept), custom_call_target="tpu_custom_call" | custom-call | tf_op jit(solution)/shard_map/finish/pallas_call | solution.py:26
Async XLA Ops:
  2.1 6.5 %collective-permute-start = (f32[248,128]{1,0:T(8,128)S(1)}, f32[248,128]{1,0:T(8,128)S(1)}, u32[]{:S(2)}, u32[]{:S(2)}) collective-permute-start(f32[248,128]{1,0:T(8,128)S(1)} %get-tuple-element.20), channel_id=1, source_target_pairs={{0,8},{16,24},{8,0},{24,16},{1,9},{17,25},{9,1},{25,17},{2,10},{18... | collective-permute-start | bytes 380936 | tf_op jit(solution)/shard_map/ppermute | solution.py:602
  5.2 3.4 %collective-permute-start.1 = (f32[248,128]{1,0:T(8,128)S(1)}, f32[248,128]{1,0:T(8,128)S(1)}, u32[]{:S(2)}, u32[]{:S(2)}) collective-permute-start(f32[248,128]{1,0:T(8,128)S(1)} %get-tuple-element.21), channel_id=1, source_target_pairs={{8,16},{16,8},{9,17},{17,9},{10,18},{18,10},{11,19},{19,11},{12,20... | collective-permute-start | bytes 380936 | tf_op jit(solution)/shard_map/ppermute | solution.py:602
  8.8 8.1 %collective-permute-start.2 = (f32[320,128]{1,0:T(8,128)S(1)}, f32[320,128]{1,0:T(8,128)S(1)}, u32[]{:S(2)}, u32[]{:S(2)}) collective-permute-start(f32[320,128]{1,0:T(8,128)S(1)} %get-tuple-element.25), channel_id=1, source_target_pairs={{0,1},{2,3},{4,5},{6,7},{1,0},{3,2},{5,4},{7,6},{8,9},{10,11},{12,... | collective-permute-start | bytes 491528 | tf_op jit(solution)/shard_map/ppermute | solution.py:602
  8.9 8.0 %collective-permute-start.3 = (f32[320,128]{1,0:T(8,128)S(1)}, f32[320,128]{1,0:T(8,128)S(1)}, u32[]{:S(2)}, u32[]{:S(2)}) collective-permute-start(f32[320,128]{1,0:T(8,128)S(1)} %get-tuple-element.26), channel_id=1, source_target_pairs={{1,2},{3,4},{5,6},{7,0},{2,1},{4,3},{6,5},{0,7},{9,10},{11,12},{13... | collective-permute-start | bytes 491528 | tf_op jit(solution)/shard_map/ppermute | solution.py:602
  11.6 13.7 %collective-permute-start.4 = (f32[304,128]{1,0:T(8,128)S(1)}, f32[304,128]{1,0:T(8,128)S(1)}, u32[]{:S(2)}, u32[]{:S(2)}) collective-permute-start(f32[304,128]{1,0:T(8,128)S(1)} %get-tuple-element.31), channel_id=1, source_target_pairs={{0,8},{16,24},{8,0},{24,16},{1,9},{17,25},{9,1},{25,17},{2,10},{18... | collective-permute-start | bytes 466952 | tf_op jit(solution)/shard_map/ppermute | solution.py:602
  16.2 9.1 %collective-permute-start.5 = (f32[304,128]{1,0:T(8,128)S(1)}, f32[304,128]{1,0:T(8,128)S(1)}, u32[]{:S(2)}, u32[]{:S(2)}) collective-permute-start(f32[304,128]{1,0:T(8,128)S(1)} %get-tuple-element.32), channel_id=1, source_target_pairs={{8,16},{16,8},{9,17},{17,9},{10,18},{18,10},{11,19},{19,11},{12,20... | collective-permute-start | bytes 466952 | tf_op jit(solution)/shard_map/ppermute | solution.py:602
  18.9 13.5 %all-to-all-start = ((f32[32,1,128]{2,1,0:T(1,128)}), f32[32,1,128]{2,1,0:T(1,128)S(1)}, u32[]{:S(2)}, u32[]{:S(2)}) async-start(f32[32,1,128]{2,1,0:T(1,128)} %get-tuple-element.27), calls=%async_computation | async-start | bytes 32768 | tf_op jit(solution)/shard_map/all_to_all | solution.py:656
